TPU v7x, 128 devices: a whole 4x4x4 slice. The times are simulated.
128 devices in a mesh: neg: 16 (over x, y), qry: 8 (over z, core).
Axes of the slice: x: 4, y: 4, z: 4, core: 2. Of those that a mesh axis runs over, the one named last changes fastest.
Arguments:
- items_table: bfloat16 [131072, 512], P('neg'), may hold values from -6 to 6
- fetch_rows: int32 [2048, 640], P(('neg', 'qry')), may hold values from 0 to 8191, as said below
- neighbour_slots: int32 [65536, 40], P(('neg', 'qry')), may hold values from 0 to 10239, as said below
- neighbour_count: int32 [65536], P(('neg', 'qry')), may hold values from 20 to 40
- self_slot: int32 [65536], P(('neg', 'qry')), may hold values from 0 to 10239
- negative_count: int32 [65536], P('neg'), may hold values from 1 to 999
- message_weight: bfloat16 [512, 512], replicated, may hold values from -0.25 to 0.25
- message_bias: float32 [512], replicated, may hold values from -3 to 3
- self_weight: bfloat16 [512, 512], replicated, may hold values from -0.25 to 0.25
- neighbour_weight: bfloat16 [512, 512], replicated, may hold values from -0.25 to 0.25
- output_bias: float32 [512], replicated, may hold values from -3 to 3
- queries: bfloat16 [8192, 512], P('qry'), may hold values from -8 to 8
Outputs:
- negative_embed: bfloat16 [65536, 512], P(('neg', 'qry'))
- query_lse: float32 [8192], P('qry')
Inputs may be any that keep to these rules, and one draw needn't show every extreme that they name: Within one row of fetch_rows (one device's list for one partition) no item appears twice. `neighbour_slots`: every one of a device's 16 * 640 fetched rows is named by at least one live neighbour of that device's negatives.
All inputs are finite; a program needn't handle non-finite values.
Results may differ from a plain program's by a relative error of at most 0.0055.
Values may be sent and summed in bfloat16 or wider, within the bound.
A program may use at most 128 MiB of HBM per device.

v0:
```python
import math

import jax
import jax.numpy as jnp
from jax import lax
from jax.sharding import PartitionSpec as P


def from_everyone(x, axis):
    devices = lax.axis_size(axis)
    return lax.all_to_all(jnp.broadcast_to(x[None], (devices, *x.shape)), axis, 0, 0, tiled=True)


def gathered_once(x, axis):
    leaves = jax.tree.leaves(x)
    sequence = sorted(range(len(leaves)), key=lambda k: -leaves[k].size)
    width = (1, *leaves[sequence[0]].shape)[-1]
    lines = [
        jnp.pad(leaves[k].reshape(-1), (0, -leaves[k].size % width)).reshape(-1, width)
        for k in sequence
    ]
    both, at, found = (from_everyone(jnp.concatenate(lines), axis), 0, {})
    for k, line in zip(sequence, lines):
        slab = both[:, at : at + len(line)].reshape(len(both), -1)
        found[k] = slab[:, : leaves[k].size].reshape(-1, *leaves[k].shape)
        at += len(line)
    numbers = iter(range(len(leaves)))
    return jax.tree.map(lambda _: found[next(numbers)], x)


def joined_by_halves(pieces, combine):
    while len(jax.tree.leaves(pieces)[0]) > 1:
        pieces = jax.vmap(combine)(
            *(jax.tree.map(lambda part: part[side::2], pieces) for side in (0, 1))
        )
    return jax.tree.map(lambda part: part[0], pieces)


def merged(x, axis, combine):
    pieces = gathered_once(x, axis)
    return joined_by_halves(pieces, combine)


def pair_join(first, second):
    top_value = jnp.maximum(first[0], second[0])
    return (
        top_value,
        first[1] * jnp.exp(first[0] - top_value) + second[1] * jnp.exp(second[0] - top_value),
    )


def combine_column(peak, totals):
    return merged((peak, totals), "neg", pair_join)


def score_against(query_part, negative_part):
    return lax.dot_general(
        query_part, negative_part, (((1,), (1,)), ((), ())), preferred_element_type=jnp.float32
    )


def make_message(rows, message_weight, message_bias):
    return jax.nn.relu(
        jnp.dot(rows, message_weight, preferred_element_type=jnp.float32) + message_bias
    ).astype(jnp.bfloat16)


def per_device(
    items_table,
    fetch_rows,
    neighbour_slots,
    neighbour_count,
    self_slot,
    negative_count,
    message_weight,
    message_bias,
    self_weight,
    neighbour_weight,
    output_bias,
    queries,
):
    width = items_table.shape[1]
    neighbours = neighbour_slots.shape[1]
    live_mask = jnp.arange(neighbours, dtype=jnp.int32)[None, :] < neighbour_count[:, None]
    served = items_table[lax.all_to_all(fetch_rows, "neg", split_axis=0, concat_axis=0, tiled=True)]
    fetched = lax.all_to_all(served, "neg", split_axis=0, concat_axis=0, tiled=True)
    fetched = fetched.reshape(-1, width)
    message = make_message(fetched, message_weight, message_bias)
    gathered = message[neighbour_slots]
    summed = jnp.sum(
        jnp.where(live_mask[:, :, None], gathered, jnp.zeros((), jnp.bfloat16)),
        axis=1,
        dtype=jnp.float32,
    )
    self_rows = fetched[self_slot]
    neighbour_mean = (summed / neighbour_count.astype(jnp.float32)[:, None]).astype(jnp.bfloat16)
    hidden = jnp.dot(self_rows, self_weight, preferred_element_type=jnp.float32)
    hidden = (
        hidden
        + jnp.dot(neighbour_mean, neighbour_weight, preferred_element_type=jnp.float32)
        + output_bias
    )
    hidden = jax.nn.relu(hidden)
    scale_inv = lax.rsqrt(jnp.mean(hidden * hidden, axis=-1, keepdims=True) + 0.25)
    negative_embed = (hidden * scale_inv).astype(jnp.bfloat16)
    log_count = jnp.log(negative_count.astype(jnp.float32))
    negatives_all = log_count.shape[0] * lax.axis_size("neg")
    query_rows_own = queries.shape[0]
    peak_old = jnp.full((query_rows_own,), -1e30, jnp.float32)
    scores = (
        0.25 * score_against(queries, lax.all_gather(negative_embed, "qry", axis=0, tiled=True))
        - log_count[None, :]
    )
    peak_new = jnp.maximum(peak_old, jnp.max(scores, axis=1))
    totals_new = jnp.sum(jnp.exp(scores - peak_new[:, None]), axis=1)
    peak = peak_new
    totals = totals_new
    peak, totals = combine_column(peak, totals)
    query_lse = peak + jnp.log(totals) - math.log(negatives_all)
    return (negative_embed, query_lse)


def solution(mesh):
    in_specs = (
        P("neg", None),
        P(("neg", "qry"), None),
        P(("neg", "qry"), None),
        P(("neg", "qry")),
        P(("neg", "qry")),
        P("neg"),
        P(),
        P(),
        P(),
        P(),
        P(),
        P("qry", None),
    )
    out_specs = (P(("neg", "qry"), None), P("qry"))
    return jax.shard_map(
        per_device, mesh=mesh, in_specs=in_specs, out_specs=out_specs, check_vma=False
    )
```

profile of v0, /device:TPU:1, one launch (start us, length us, event | category | flops | bytes accessed | tf_op | source)
XLA Modules:
  0.0 450.2 jit_solution(16907306595817737772)
XLA Ops:
  7.2 0.0 copy-start
  7.2 0.9 all_to_all.14
  8.1 13.9 %all_to_all.22 = s32[16,1,640]{2,1,0:T(1,128)S(1)} all-to-all(s32[16,1,640]{2,1,0:T(1,128)S(1)} %all_to_all.14), channel_id=1, replica_groups=mesh['neg'=16,'qry'=8] {'neg'}, dimensions={0} | all-to-all | bytes 81920 | tf_op jit(solution)/shard_map/all_to_all | solution.py:85
  22.0 46.5 %gather_fusion = bf16[10240,512]{1,0:T(8,128)(2,1)} fusion(bf16[8192,512]{1,0:T(8,128)(2,1)} %param.12, s32[10240]{0:T(1024)S(1)} %broadcast_clamp_fusion.1), kind=kCustom, calls=%fused_computation | custom fusion | bytes 21012480 | tf_op jit(solution)/shard_map/gather | solution.py:85
  68.5 0.0 copy-start.3
  68.5 0.0 copy-start.5
  68.5 0.0 copy-start.6
  68.5 0.0 copy-start.2
  68.6 0.0 copy-start.8
  68.6 5.0 %all-to-all-start.1 = ((bf16[16,640,512]{2,1,0:T(8,128)(2,1)}), bf16[16,640,512]{2,1,0:T(8,128)(2,1)}, u32[]{:S(2)}, u32[]{:S(2)}) async-start(bf16[16,640,512]{2,1,0:T(8,128)(2,1)} %bitcast.21), calls=%async_computation.1 | async-start | bytes 20971520 | tf_op jit(solution)/shard_map/all_to_all | solution.py:86
  73.6 0.0 all-gather.2.cloned.1.call-start
  73.6 0.0 copy-done.3
  73.6 0.1 copy.19
  73.8 0.2 reshape.119
  74.0 0.0 copy-done.5
  74.0 0.0 copy-done.6
  74.0 0.1 iota_compare_fusion
  74.2 173.9 %all-to-all-done.1 = bf16[16,640,512]{2,1,0:T(8,128)(2,1)} async-done(((bf16[16,640,512]{2,1,0:T(8,128)(2,1)}), bf16[16,640,512]{2,1,0:T(8,128)(2,1)}, u32[]{:S(2)}, u32[]{:S(2)}) %all-to-all-start.1) | async-done | bytes 10485792 | tf_op jit(solution)/shard_map/all_to_all | solution.py:86
  248.1 7.5 %gather_fusion.1 = bf16[512,512]{1,0:T(8,128)(2,1)S(1)} fusion(bf16[10240,512]{1,0:T(8,128)(2,1)} %bitcast.3, s32[1024]{0:T(1024)S(1)} %pad_clamp_fusion), kind=kCustom, calls=%fused_computation.1 | custom fusion | bytes 1050624 | tf_op jit(solution)/shard_map/gather | solution.py:95
  255.6 0.0 copy-done.2
  255.6 0.5 fusion.7
  256.1 0.0 copy-done.8
  256.1 10.8 %maximum_convert_fusion = bf16[10240,512]{1,0:T(8,128)(2,1)} fusion(bf16[10240,512]{1,0:T(8,128)(2,1)} %bitcast.3, bf16[512,512]{1,0:T(8,128)(2,1)} %param.18, f32[512]{0:T(512)S(1)} %copy-done.8), kind=kOutput, calls=%fused_computation.4 | convolution fusion | flops 5384437760 | bytes 21497856 | tf_op jit(solution)/shard_map/dot_general | solution.py:64
  266.9 88.5 %gather_fusion.2 = bf16[20480,512]{1,0:T(8,128)(2,1)} fusion(bf16[10240,512]{1,0:T(8,128)(2,1)} %maximum_convert_fusion, s32[20480]{0:T(1024)S(1)} %broadcast_clamp_fusion), kind=kCustom, calls=%fused_computation.2 | custom fusion | bytes 42024960 | tf_op jit(solution)/shard_map/gather | solution.py:89
  355.4 0.0 copy-start.7
  355.4 0.0 copy-start.9
  355.4 0.0 copy-start.4
  355.4 17.6 %convert_reduce_fusion = f32[512,512]{1,0:T(8,128)S(1)} fusion(bf16[512,40,512]{2,1,0:T(8,128)(2,1)} %bitcast.20, pred[512,40]{1,0:T(8,128)(4,1)S(1)} %iota_compare_fusion), kind=kLoop, calls=%fused_computation.3 | loop fusion | flops 31195136 | bytes 22040576 | tf_op jit(solution)/shard_map/reduce_sum | solution.py:90
  373.1 0.0 copy-done.7
  373.1 0.0 copy-done.9
  373.1 0.6 multiply_reduce_fusion
  373.7 0.9 multiply_convert_fusion
  374.6 0.0 all-gather.2.cloned.1.call-update
  374.7 0.0 copy-done.4
  374.7 41.5 %all-gather.2.cloned.1.call-done = bf16[4096,512]{0,1:T(8,128)(2,1)} async-done(((bf16[512,512]{0,1:T(8,128)(2,1)}), bf16[4096,512]{0,1:T(8,128)(2,1)}) %all-gather.2.cloned.1.call-update) | async-done | bytes 4194320 | tf_op jit(solution)/shard_map/all_gather | solution.py:111
  416.2 0.0 copy-done
  416.2 8.4 %fusion = (f32[1024]{0:T(1024)S(1)}, f32[4096,1024]{1,0:T(8,128)S(1)}) fusion(f32[4096]{0:T(1024)S(1)} %convert_log_fusion, bf16[4096,512]{0,1:T(8,128)(2,1)} %all-gather.2.cloned.1.call-done, bf16[1024,512]{1,0:T(8,128)(2,1)S(1)} %copy-done), kind=kOutput, calls=%fused_computation.7 | convolution fusion | flops 4307549184 | bytes 22040576 | tf_op jit(solution)/shard_map/dot_general | solution.py:57
  424.6 0.0 copy-start.1
  424.6 3.6 exponential_reduce_fusion
  428.2 0.7 broadcast_in_dim.42
  428.9 6.5 %all-to-all-start.2 = ((f32[16,2,1024]{2,1,0:T(2,128)}), f32[16,2,1024]{2,1,0:T(2,128)S(1)}, u32[]{:S(2)}, u32[]{:S(2)}) async-start(f32[16,2,1024]{2,1,0:T(2,128)} %broadcast_in_dim.42), calls=%async_computation.2 | async-start | bytes 262144 | tf_op jit(solution)/shard_map/all_to_all | solution.py:11
  435.5 0.0 copy-done.1
  435.5 1.0 copy.21
  436.5 5.7 %all-to-all-done.2 = f32[16,2,1024]{2,1,0:T(2,128)S(1)} async-done(((f32[16,2,1024]{2,1,0:T(2,128)}), f32[16,2,1024]{2,1,0:T(2,128)S(1)}, u32[]{:S(2)}, u32[]{:S(2)}) %all-to-all-start.2) | async-done | bytes 131104 | tf_op jit(solution)/shard_map/all_to_all | solution.py:11
  442.2 0.1 fusion.6
  442.7 0.6 add_add_fusion
  (27 shorter events, 0.5 us)
Async XLA Ops:
  7.2 409.0 %copy-start = (bf16[1024,512]{1,0:T(8,128)(2,1)S(1)}, bf16[1024,512]{1,0:T(8,128)(2,1)}, u32[]{:S(2)}) copy-start(bf16[1024,512]{1,0:T(8,128)(2,1)} %param.23) | copy-start | bytes 3145732
  68.5 5.1 %copy-start.3 = (s32[512,40]{0,1:T(8,128)S(1)}, s32[512,40]{0,1:T(8,128)}, u32[]{:S(2)}) copy-start(s32[512,40]{0,1:T(8,128)} %param.14) | copy-start | bytes 245764
  68.5 5.4 %copy-start.5 = (s32[512]{0:T(512)S(1)}, s32[512]{0:T(512)}, u32[]{:S(2)}) copy-start(s32[512]{0:T(512)} %param.15) | copy-start | bytes 6148
  68.5 5.4 %copy-start.6 = (s32[512]{0:T(512)S(1)}, s32[512]{0:T(512)}, u32[]{:S(2)}) copy-start(s32[512]{0:T(512)} %param.16) | copy-start | bytes 6148
  68.5 187.1 %copy-start.2 = (bf16[512,512]{1,0:T(8,128)(2,1)S(1)}, bf16[512,512]{1,0:T(8,128)(2,1)}, u32[]{:S(2)}) copy-start(bf16[512,512]{1,0:T(8,128)(2,1)} %param.20) | copy-start | bytes 1572868
  68.6 187.5 %copy-start.8 = (f32[512]{0:T(512)S(1)}, f32[512]{0:T(512)}, u32[]{:S(2)}) copy-start(f32[512]{0:T(512)} %param.19) | copy-start | bytes 6148
  68.6 179.5 %all-to-all-start.1 = ((bf16[16,640,512]{2,1,0:T(8,128)(2,1)}), bf16[16,640,512]{2,1,0:T(8,128)(2,1)}, u32[]{:S(2)}, u32[]{:S(2)}) async-start(bf16[16,640,512]{2,1,0:T(8,128)(2,1)} %bitcast.21), calls=%async_computation.1 | async-start | bytes 20971520 | tf_op jit(solution)/shard_map/all_to_all | solution.py:86
  73.6 342.6 %all-gather.2.cloned.1.call-start = ((), (), s32[]{:S(2)}) async-start(), calls=%async_computation.3 | async-start | bytes 4718592 | tf_op jit(solution)/shard_map/all_gather | solution.py:111
  355.4 17.7 %copy-start.7 = (bf16[512,512]{1,0:T(8,128)(2,1)S(1)}, bf16[512,512]{1,0:T(8,128)(2,1)}, u32[]{:S(2)}) copy-start(bf16[512,512]{1,0:T(8,128)(2,1)} %param.21) | copy-start | bytes 1572868
  355.4 17.7 %copy-start.9 = (f32[512]{0:T(512)S(1)}, f32[512]{0:T(512)}, u32[]{:S(2)}) copy-start(f32[512]{0:T(512)} %param.22) | copy-start | bytes 6148
  355.4 19.3 %copy-start.4 = (s32[4096]{0:T(1024)S(1)}, s32[4096]{0:T(1024)}, u32[]{:S(2)}) copy-start(s32[4096]{0:T(1024)} %param.17) | copy-start | bytes 49156
  424.6 10.9 %copy-start.1 = (bf16[512,512]{0,1:T(8,128)(2,1)S(1)}, bf16[512,512]{0,1:T(8,128)(2,1)}, u32[]{:S(2)}) copy-start(bf16[512,512]{0,1:T(8,128)(2,1)} %multiply_convert_fusion) | copy-start | bytes 1572868
  428.9 13.2 %all-to-all-start.2 = ((f32[16,2,1024]{2,1,0:T(2,128)}), f32[16,2,1024]{2,1,0:T(2,128)S(1)}, u32[]{:S(2)}, u32[]{:S(2)}) async-start(f32[16,2,1024]{2,1,0:T(2,128)} %broadcast_in_dim.42), calls=%async_computation.2 | async-start | bytes 262144 | tf_op jit(solution)/shard_map/all_to_all | solution.py:11
Sparse Core Ops, SparseCore 0:
  374.8 41.3 all-gather.1
where the time goes:
time: 451 us; the launch traced here: 450 us
  waiting for transfers between devices  221 us (49%)
  local copies, waits for them, and re-layouts  146 us (32%)
  other arithmetic  23.1 us (5%)
  matrix products  20.3 us (5%)
  between operations  14.3 us (3%)
  blocking collectives  13.9 us (3%)
  starting transfers between devices  11.6 us (3%)
    all_to_all x1, waiting for transfers between devices, per_device(): lax.all_to_all(served, 'neg', split_axis=0, concat_axis=0, tiled=True)  174 us
    gather x1, local copies, waits for them, and re-layouts, per_device(): gathered = message[neighbour_slots]  88.5 us
    gather x1, local copies, waits for them, and re-layouts, per_device(): items_table[lax.all_to_all(fetch_rows, 'neg', split_axis=0, concat_axis=0...  46.5 us
    all_gather x1, waiting for transfers between devices, per_device(): lax.all_gather(negative_embed, 'qry', axis=0, tiled=True)  41.5 us
    reduce_sum x1, other arithmetic, per_device(): jnp.sum(jnp.where(live_mask[:, :, None], gathered, jnp.zeros((), jnp.bflo...  17.6 us
    all_to_all x1, blocking collectives, per_device(): lax.all_to_all(fetch_rows, 'neg', split_axis=0, concat_axis=0, tiled=True)  13.9 us
    dot_general x1, matrix products, make_message(): jnp.dot(rows, message_weight, preferred_element_type=jnp.float32)  10.8 us
  transfers between devices with their start and end apart: 3, of which 3 were waited for; matrix products, arithmetic and copies ran while one was open for 0% of the time, Pallas kernels for 0%

commit v1 on v0

v1 whole, which is shorter than its diff:
```python
import functools
import math

import jax
import jax.numpy as jnp
from jax import lax
from jax.experimental import pallas as pl
from jax.experimental.pallas import tpu as pltpu
from jax.sharding import PartitionSpec as P

MESH = pl.DeviceIdType.MESH
VMEM = pl.BlockSpec(memory_space=pltpu.VMEM)


def greet(peers):
    barrier = pltpu.get_barrier_semaphore()
    for peer in peers:
        pl.semaphore_signal(barrier, inc=1, device_id=peer, device_id_type=MESH)
    pl.semaphore_wait(barrier, len(peers))


def remote(src, dst, send, recv, peer):
    return pltpu.make_async_remote_copy(
        src_ref=src, dst_ref=dst, send_sem=send, recv_sem=recv, device_id=peer, device_id_type=MESH
    )


def index_kernel(rows_ref, slots_ref, last_ref, rows_out, aux_out, aux_own, send_sem, recv_sem):
    me = lax.axis_index("neg")
    peers = [{"neg": lax.rem(me + d, 16)} for d in range(1, 16)]
    count = lax.shift_right_logical(last_ref[...], 16)
    for h in range(2):
        ks = lax.broadcasted_iota(jnp.int32, (20, 512), 0) + 20 * h
        half = jnp.where(ks < count, slots_ref[20 * h:20 * h + 20, :], 0xFFFF)
        if h == 0:
            low = half
        else:
            aux_own[0:20, :] = low | jnp.left_shift(half, 16)
    aux_own[20:24, :] = jnp.broadcast_to(last_ref[...], (4, 512))
    greet(peers)
    copies = []
    for d, peer in enumerate(peers):
        other = lax.rem(me + d + 1, 16)
        copies.append(remote(rows_ref.at[other], rows_out.at[me], send_sem.at[0, d], recv_sem.at[0, d], peer))
    for d, peer in enumerate(peers):
        copies.append(remote(aux_own, aux_out.at[me], send_sem.at[1, d], recv_sem.at[1, d], peer))
    for copy in copies:
        copy.start()
    rows_out[me] = rows_ref[me]
    aux_out[me] = aux_own[...]
    for copy in copies:
        copy.wait()


def exchange_indices(fetch_rows, slots, last):
    return pl.pallas_call(
        index_kernel,
        out_shape=(
            jax.ShapeDtypeStruct((16, 1, 640), jnp.int32),
            jax.ShapeDtypeStruct((16, 24, 512), jnp.int32),
        ),
        in_specs=[VMEM] * 3,
        out_specs=(VMEM, VMEM),
        scratch_shapes=[
            pltpu.VMEM((24, 512), jnp.int32),
            pltpu.SemaphoreType.DMA((2, 15)),
            pltpu.SemaphoreType.DMA((2, 15)),
        ],
        compiler_params=pltpu.CompilerParams(collective_id=1, has_side_effects=True),
        name="exchange_indices",
    )(fetch_rows, slots, last)


def partial_kernel(get_p, rows_ref, aux_ref, table_ref, wm_ref, ws_ref, wn_ref, bm_ref, out_ref,
                   t_ref, tbuf, g_ref, gb_ref, c_ref, key_ref, val_ref, self_ref, rcnt_ref, pbuf, in_sem, out_sem):
    p = get_p()
    blocks = 16
    blk = 512

    def fetch(i, slot):
        return pltpu.make_async_copy(table_ref.at[pl.ds(i * blk, blk), :], tbuf.at[slot], in_sem.at[slot])

    fetch(0, 0).start()

    def build(i, _):
        slot = lax.rem(i, 2)

        @pl.when(i + 1 < blocks)
        def _():
            fetch(i + 1, 1 - slot).start()
        fetch(i, slot).wait()
        x = tbuf[slot]
        m = jnp.dot(x, wm_ref[...], preferred_element_type=jnp.float32) + bm_ref[...]
        m = jnp.maximum(m, 0.0).astype(jnp.bfloat16)
        t1 = jnp.dot(m, wn_ref[...], preferred_element_type=jnp.float32)
        t2 = jnp.dot(x, ws_ref[...], preferred_element_type=jnp.float32)
        base = pl.multiple_of(i * (blk * 8), 8)
        for j in range(4):
            t_ref[pl.ds(base + j, blk, stride=8), :] = t1[:, j * 128:(j + 1) * 128]
            t_ref[pl.ds(base + 4 + j, blk, stride=8), :] = t2[:, j * 128:(j + 1) * 128]
        return 0
    lax.fori_loop(0, blocks, build, 0)

    last = aux_ref[:, 20, :]
    last = jnp.concatenate([last] * 8, axis=0)
    self_ref[...] = (last & 0xFFFF).T
    rcnt_ref[...] = (1.0 / (last >> 16).astype(jnp.float32)).T

    lane = lax.broadcasted_iota(jnp.int32, (128, 128), 1)
    sub = lax.broadcasted_iota(jnp.int32, (128, 128), 0)

    def one(n, _):
        slot = lax.rem(n, 2)

        def gather(i, _):
            for u in range(32):
                s = i * 32 + u
                r = rows_ref[n, s]
                g_ref[pl.ds(pl.multiple_of(s * 8, 8), 8), :] = t_ref[pl.ds(pl.multiple_of(r * 8, 8), 8), :]
            return 0
        lax.fori_loop(0, 20, gather, 0)
        for j in range(8):
            gb_ref[:, j * 128:(j + 1) * 128] = g_ref[pl.ds(j, 640, stride=8), :].astype(jnp.bfloat16)
        packed = aux_ref[n][:24]
        for h, slots in enumerate((packed & 0xFFFF, lax.shift_right_logical(packed, 16))):
            rel = slots - 640 * p
            ok = (rel >= 0) & (rel < 640)
            key_ref[h * 24:(h + 1) * 24, :] = rel & 127
            val_ref[h * 24:(h + 1) * 24, :] = jnp.where(ok, jnp.left_shift(1, 6 * (lax.shift_right_logical(rel, 7) & 7) & 31), 0)
        for vb in range(4):
            cols = pl.ds(vb * 128, 128)
            acc = jnp.zeros((128, 128), jnp.int32)
            for k in range(40):
                kk = k if k < 20 else k + 4
                key = jnp.broadcast_to(key_ref[kk:kk + 1, cols], (128, 128))
                val = jnp.broadcast_to(val_ref[kk:kk + 1, cols], (128, 128))
                acc = acc + jnp.where(sub == key, val, 0)
            ct = acc.T
            here = lane == n
            self_col = jnp.sum(jnp.where(here, self_ref[cols, :].astype(jnp.float32), 0.0), axis=1, keepdims=True).astype(jnp.int32) - 640 * p
            for f in range(5):
                c_ref[cols, f * 128:(f + 1) * 128] = (lax.shift_right_logical(ct, 6 * f) & 63).astype(jnp.float32).astype(jnp.bfloat16)
                c_ref[cols, 640 + f * 128:640 + (f + 1) * 128] = jnp.where(self_col == lane + f * 128, 1.0, 0.0).astype(jnp.bfloat16)
        here = lax.broadcasted_iota(jnp.int32, (512, 128), 1) == n
        rcnt = jnp.sum(jnp.where(here, rcnt_ref[...], 0.0), axis=1, keepdims=True)
        part = jnp.dot(c_ref[:, :640], gb_ref[:, :512], preferred_element_type=jnp.float32) * rcnt
        part = part + jnp.dot(c_ref[:, 640:], gb_ref[:, 512:], preferred_element_type=jnp.float32)

        def send(slot, n):
            return pltpu.make_async_copy(pbuf.at[slot], out_ref.at[n], out_sem.at[slot])

        @pl.when(n >= 2)
        def _():
            send(slot, n - 2).wait()
        pbuf[slot] = part.astype(jnp.bfloat16)
        send(slot, n).start()
        return 0
    lax.fori_loop(0, 16, one, 0)
    for slot in range(2):
        pltpu.make_async_copy(pbuf.at[slot], out_ref.at[14 + slot], out_sem.at[slot]).wait()


def partials(get_p, rows, aux, table, wm, ws, wn, bm):
    vmem = pl.BlockSpec(memory_space=pltpu.VMEM)
    return pl.pallas_call(
        functools.partial(partial_kernel, get_p),
        out_shape=jax.ShapeDtypeStruct((16, 512, 512), jnp.bfloat16),
        in_specs=[pl.BlockSpec(memory_space=pltpu.SMEM), vmem, pl.BlockSpec(memory_space=pl.ANY), vmem, vmem, vmem, vmem],
        out_specs=pl.BlockSpec(memory_space=pl.ANY),
        scratch_shapes=[
            pltpu.VMEM((65536, 128), jnp.float32),
            pltpu.VMEM((2, 512, 512), jnp.bfloat16),
            pltpu.VMEM((5120, 128), jnp.float32),
            pltpu.VMEM((640, 1024), jnp.bfloat16),
            pltpu.VMEM((512, 1280), jnp.bfloat16),
            pltpu.VMEM((48, 512), jnp.int32),
            pltpu.VMEM((48, 512), jnp.int32),
            pltpu.VMEM((512, 128), jnp.int32),
            pltpu.VMEM((512, 128), jnp.float32),
            pltpu.VMEM((2, 512, 512), jnp.bfloat16),
            pltpu.SemaphoreType.DMA((2,)),
            pltpu.SemaphoreType.DMA((2,)),
        ],
        compiler_params=pltpu.CompilerParams(vmem_limit_bytes=60 * 1024 * 1024),
        cost_estimate=pl.CostEstimate(flops=24_000_000_000, bytes_accessed=24_000_000, transcendentals=0),
        name="partials",
    )(rows, aux, table, wm, ws, wn, bm)


def reduce_kernel(p_ref, out_ref, near, far, carry, total, near2, far2, carry2, send_sem, recv_sem):
    me = lax.axis_index("neg")
    spot = (me // 4, lax.rem(me, 4))

    def device(axis, step):
        moved = lax.rem(spot[axis] + step + 4, 4)
        return {"neg": moved * 4 + spot[1] if axis == 0 else spot[0] * 4 + moved}

    greet([device(axis, step) for axis in range(2) for step in (1, -1)])
    base = (0, 256)

    def block(half, dest, lo, size):
        rows = pl.ds(base[half] + lo, size)
        return p_ref.at[dest, :, rows, :] if half == 0 else p_ref.at[:, dest, rows, :]

    first = {}
    for half in range(2):
        across = lax.rem(spot[half] + 2, 4)
        for w, step in enumerate((1, -1)):
            peer = device(half, step)
            first[half, w, 0] = remote(
                block(half, across, 128 * w, 128), near.at[half, w],
                send_sem.at[0, half, w, 0], recv_sem.at[0, half, w, 0], peer)
            dest = lax.rem(spot[half] + step + 4, 4)
            first[half, w, 1] = remote(
                block(half, dest, 128 * (1 - w), 128), far.at[half, w, 1],
                send_sem.at[0, half, w, 1], recv_sem.at[0, half, w, 1], peer)
            first[half, w, 2] = remote(
                carry.at[half, w], far.at[half, w, 0],
                send_sem.at[0, half, w, 2], recv_sem.at[0, half, w, 2], peer)
    for stage in range(2):
        for half in range(2):
            for w in range(2):
                first[half, w, stage].start()
    for half in range(2):
        for w, step in enumerate((1, -1)):
            first[half, w, 0].wait_recv()
            dest = lax.rem(spot[half] + step + 4, 4)
            for j in range(4):
                own = block(half, dest, 128 * w, 128)[j]
                carry[half, w, j] = (own.astype(jnp.float32) + near[half, w, j].astype(jnp.float32)).astype(jnp.bfloat16)
            first[half, w, 2].start()
    for half in range(2):
        for w in range(2):
            first[half, w, 1].wait_recv()
            first[half, w, 2].wait_recv()
        other = 1 - half
        home = spot[half]
        for j in range(4):
            for w in range(2):
                own = block(half, home, 128 * w, 128)[j]
                value = own.astype(jnp.float32) + far[half, w, 0, j].astype(jnp.float32)
                value = value + far[half, 1 - w, 1, j].astype(jnp.float32)
                total[half, j, w] = value
    second = {}
    for half in range(2):
        other = 1 - half
        across = lax.rem(spot[other] + 2, 4)
        for w, step in enumerate((1, -1)):
            peer = device(other, step)
            dest = lax.rem(spot[other] + step + 4, 4)
            carry2[half, w, 0] = total[half, across, w].astype(jnp.bfloat16)
            carry2[half, w, 1] = total[half, dest, 1 - w].astype(jnp.bfloat16)
            for stage, target in ((0, near2.at[half, w]), (1, far2.at[half, w, 1]), (2, far2.at[half, w, 0])):
                second[half, w, stage] = remote(
                    carry2.at[half, w, stage], target,
                    send_sem.at[1, half, w, stage], recv_sem.at[1, half, w, stage], peer)
            second[half, w, 0].start()
            second[half, w, 1].start()
    for half in range(2):
        other = 1 - half
        for w, step in enumerate((1, -1)):
            second[half, w, 0].wait_recv()
            dest = lax.rem(spot[other] + step + 4, 4)
            carry2[half, w, 2] = (total[half, dest, w] + near2[half, w].astype(jnp.float32)).astype(jnp.bfloat16)
            second[half, w, 2].start()
    for half in range(2):
        home = spot[1 - half]
        for w in range(2):
            second[half, w, 1].wait_recv()
            second[half, w, 2].wait_recv()
        for w in range(2):
            value = total[half, home, w] + far2[half, w, 0].astype(jnp.float32)
            value = value + far2[half, 1 - w, 1].astype(jnp.float32)
            out_ref[pl.ds(base[half] + 128 * w, 128), :] = value
    for copies in (first, second):
        for copy in copies.values():
            copy.wait_send()


def reduce_partials(partial):
    return pl.pallas_call(
        reduce_kernel,
        out_shape=jax.ShapeDtypeStruct((512, 512), jnp.float32),
        in_specs=[VMEM],
        out_specs=VMEM,
        scratch_shapes=[
            pltpu.VMEM((2, 2, 4, 128, 512), jnp.bfloat16),
            pltpu.VMEM((2, 2, 2, 4, 128, 512), jnp.bfloat16),
            pltpu.VMEM((2, 2, 4, 128, 512), jnp.bfloat16),
            pltpu.VMEM((2, 4, 2, 128, 512), jnp.float32),
            pltpu.VMEM((2, 2, 128, 512), jnp.bfloat16),
            pltpu.VMEM((2, 2, 2, 128, 512), jnp.bfloat16),
            pltpu.VMEM((2, 2, 3, 128, 512), jnp.bfloat16),
            pltpu.SemaphoreType.DMA((2, 2, 2, 3)),
            pltpu.SemaphoreType.DMA((2, 2, 2, 3)),
        ],
        compiler_params=pltpu.CompilerParams(
            collective_id=2, has_side_effects=True, vmem_limit_bytes=48 * 1024 * 1024),
        name="reduce_partials",
    )(partial.reshape(4, 4, 512, 512))


def score_kernel(pre_ref, bias_ref, logc_ref, queries_ref, embed_ref, stats_ref, scaled):
    @pl.when(pl.program_id(0) == 0)
    def _():
        hidden = jnp.maximum(pre_ref[...] + bias_ref[...], 0.0)
        inv = lax.rsqrt(jnp.mean(hidden * hidden, axis=-1, keepdims=True) + 0.25)
        embed = (hidden * inv).astype(jnp.bfloat16)
        embed_ref[...] = embed
        scaled[...] = embed * jnp.bfloat16(0.25)
    for part in range(2):
        cols = pl.ds(part * 512, 512)
        scores = lax.dot_general(
            scaled[...], queries_ref[cols, :], (((1,), (1,)), ((), ())), preferred_element_type=jnp.float32
        ) - logc_ref[...]
        peak = jnp.max(scores, axis=0, keepdims=True)
        total = jnp.sum(jnp.exp(scores - peak), axis=0, keepdims=True)
        stats_ref[0, 0:1, cols] = peak
        stats_ref[0, 1:2, cols] = total


def score(pre, bias, log_count, queries):
    return pl.pallas_call(
        score_kernel,
        grid=(8,),
        out_shape=(
            jax.ShapeDtypeStruct((512, 512), jnp.bfloat16),
            jax.ShapeDtypeStruct((8, 2, 1024), jnp.float32),
        ),
        in_specs=[
            pl.BlockSpec((512, 512), lambda i: (0, 0)),
            pl.BlockSpec((1, 512), lambda i: (0, 0)),
            pl.BlockSpec((512, 1), lambda i: (0, 0)),
            pl.BlockSpec((1024, 512), lambda i: (i, 0)),
        ],
        out_specs=(
            pl.BlockSpec((512, 512), lambda i: (0, 0)),
            pl.BlockSpec((1, 2, 1024), lambda i: (i, 0, 0)),
        ),
        scratch_shapes=[pltpu.VMEM((512, 512), jnp.bfloat16)],
        compiler_params=pltpu.CompilerParams(dimension_semantics=("arbitrary",), vmem_limit_bytes=32 * 1024 * 1024),
        name="score",
    )(pre, bias, log_count, queries)


def joined(stats):
    peak = jnp.max(stats[:, 0:1, :], axis=0)
    total = jnp.sum(stats[:, 1:2, :] * jnp.exp(stats[:, 0:1, :] - peak[None]), axis=0)
    return peak, total


def combine_kernel(stats_ref, out_ref, got, mine, final, send_sem, recv_sem, send_sem2, recv_sem2):
    q = lax.axis_index("qry")
    n = lax.axis_index("neg")
    row_peers = [{"qry": lax.rem(q + d, 8)} for d in range(1, 8)]
    column_peers = [{"neg": lax.rem(n + d, 16)} for d in range(1, 16)]
    greet(row_peers + column_peers)
    copies = []
    for d, peer in enumerate(row_peers):
        copies.append(remote(stats_ref.at[lax.rem(q + d + 1, 8)], got.at[q], send_sem.at[d], recv_sem.at[d], peer))
        copies[-1].start()
    got[q] = stats_ref[q]
    for copy in copies:
        copy.wait_recv()
    peak, total = joined(got[...])
    mine[...] = jnp.concatenate([peak, total], axis=0)
    final[n] = mine[...]
    for d, peer in enumerate(column_peers):
        copies.append(remote(mine, final.at[n], send_sem2.at[d], recv_sem2.at[d], peer))
        copies[-1].start()
    for copy in copies[7:]:
        copy.wait_recv()
    peak, total = joined(final[...])
    out_ref[...] = peak + jnp.log(total) - math.log(65536)
    for copy in copies:
        copy.wait_send()


def combine(stats):
    return pl.pallas_call(
        combine_kernel,
        out_shape=jax.ShapeDtypeStruct((1, 1024), jnp.float32),
        in_specs=[VMEM],
        out_specs=VMEM,
        scratch_shapes=[
            pltpu.VMEM((8, 2, 1024), jnp.float32),
            pltpu.VMEM((2, 1024), jnp.float32),
            pltpu.VMEM((16, 2, 1024), jnp.float32),
            pltpu.SemaphoreType.DMA((7,)),
            pltpu.SemaphoreType.DMA((7,)),
            pltpu.SemaphoreType.DMA((15,)),
            pltpu.SemaphoreType.DMA((15,)),
        ],
        compiler_params=pltpu.CompilerParams(collective_id=3, has_side_effects=True),
        name="combine",
    )(stats)


def per_device(
    items_table,
    fetch_rows,
    neighbour_slots,
    neighbour_count,
    self_slot,
    negative_count,
    message_weight,
    message_bias,
    self_weight,
    neighbour_weight,
    output_bias,
    queries,
):
    queries_all = lax.all_gather(queries, "qry", axis=0, tiled=True)
    last = (self_slot | jnp.left_shift(neighbour_count, 16)).reshape(1, 512)
    rows, aux = exchange_indices(fetch_rows.reshape(16, 1, 640), neighbour_slots.T, last)
    partial = partials(
        lambda: lax.axis_index("neg"), rows.reshape(16, 640), aux, items_table,
        message_weight, self_weight, neighbour_weight, message_bias.reshape(1, 512))
    pre = reduce_partials(partial)
    own_count = lax.dynamic_slice(negative_count, (lax.axis_index("qry") * 512,), (512,))
    log_count = jnp.log(own_count.astype(jnp.float32)).reshape(512, 1)
    negative_embed, stats = score(pre, output_bias.reshape(1, 512), log_count, queries_all)
    query_lse = combine(stats)
    return negative_embed, query_lse.reshape(1024)


def solution(mesh):
    in_specs = (
        P("neg", None),
        P(("neg", "qry"), None),
        P(("neg", "qry"), None),
        P(("neg", "qry")),
        P(("neg", "qry")),
        P("neg"),
        P(),
        P(),
        P(),
        P(),
        P(),
        P("qry", None),
    )
    out_specs = (P(("neg", "qry"), None), P("qry"))
    return jax.shard_map(
        per_device, mesh=mesh, in_specs=in_specs, out_specs=out_specs, check_vma=False
    )
```

time: 451 us -> 220 us (0.49)
  waiting for transfers between devices: 221 us -> 0.7 us
  Pallas kernels: 0 us -> 194 us
  local copies, waits for them, and re-layouts: 146 us -> 8.24 us
  other arithmetic: 23.1 us -> 2.04 us
  matrix products: 20.3 us -> 0 us
  blocking collectives: 13.9 us -> 0 us
  starting transfers between devices: 11.6 us -> 0.04 us
    pallas_call x0 -> x5, Pallas kernels: none -> 194 us  [the longest x1 95.2 us: partials(): pl.pallas_call(functools.partial(partial_kernel, get_p), out_shape=jax.Sh...]
    all_to_all x2 -> x0, waiting for transfers between devices: 180 us -> none  [the longest x1 174 us: per_device(): lax.all_to_all(served, 'neg', split_axis=0, concat_axis=0, tiled=True)]
    gather x3 -> x0, local copies, waits for them, and re-layouts: 143 us -> none  [the longest x1 88.5 us: per_device(): gathered = message[neighbour_slots]]
    all_gather x1, waiting for transfers between devices: 41.5 us -> 0.02 us  [per_device(): queries_all = lax.all_gather(queries, 'qry', axis=0, tiled=True)]
    reduce_sum x2 -> x0, other arithmetic: 21.2 us -> none  [the longest x1 17.6 us: per_device(): jnp.sum(jnp.where(live_mask[:, :, None], gathered, jnp.zeros((), jnp.bflo...]
    dot_general x4 -> x0, matrix products: 20.3 us -> none  [the longest x1 10.8 us: make_message(): jnp.dot(rows, message_weight, preferred_element_type=jnp.float32)]
    all_to_all x1 -> x0, blocking collectives: 13.9 us -> none  [per_device(): lax.all_to_all(fetch_rows, 'neg', split_axis=0, concat_axis=0, tiled=True)]
    all_to_all x2 -> x0, starting transfers between devices: 11.5 us -> none  [the longest x1 6.53 us: from_everyone(): lax.all_to_all(jnp.broadcast_to(x[None], (devices, *x.shape)), axis, 0, 0...]
  transfers between devices with their start and end apart: 3 -> 1, of which waited for: 3 -> 0; matrix products, arithmetic and copies ran while one was open for 0% -> 2% of each run, Pallas kernels for 0% -> 75%
where the time goes in v1:
time: 220 us; the launch traced here: 219 us
  Pallas kernels  194 us (88%)
  between operations  14.1 us (6%)
  local copies, waits for them, and re-layouts  8.24 us (4%)
    pallas_call x1, Pallas kernels, partials(): pl.pallas_call(functools.partial(partial_kernel, get_p), out_shape=jax.Sh...  95.2 us
    pallas_call x1, Pallas kernels, reduce_partials(): pl.pallas_call(reduce_kernel, out_shape=jax.ShapeDtypeStruct((512, 512),...  51 us
    pallas_call x1, Pallas kernels, combine(): pl.pallas_call(combine_kernel, out_shape=jax.ShapeDtypeStruct((1, 1024),...  20 us
    pallas_call x1, Pallas kernels, exchange_indices(): pl.pallas_call(index_kernel, out_shape=(jax.ShapeDtypeStruct((16, 1, 640)...  19.1 us
    pallas_call x1, Pallas kernels, score(): pl.pallas_call(score_kernel, grid=(8,), out_shape=(jax.ShapeDtypeStruct((...  8.86 us
    unnamed x8, local copies, waits for them, and re-layouts  6.66 us
  transfers between devices with their start and end apart: 1, of which 0 were waited for; matrix products, arithmetic and copies ran while one was open for 2% of the time, Pallas kernels for 75%

profile of v1, /device:TPU:1, one launch (start us, length us, event | category | flops | bytes accessed | tf_op | source)
XLA Modules:
  0.0 219.4 jit_solution(11469627827993572892)
XLA Ops:
  7.2 0.0 all-gather.2.cloned.1.call-start
  7.2 0.7 all-gather.2.cloned.1.call-update
  7.9 0.8 convert_log_fusion
  8.7 0.2 copy.14.logc_ref
  8.8 1.4 reshape.28.rows_ref
  10.3 1.3 shift-left_or_fusion
  11.5 19.1 %exchange_indices.1 = (s32[16,1,640]{2,1,0:T(1,128)}, s32[16,24,512]{2,1,0:T(8,128)}) custom-call(s32[16,1,640]{2,1,0:T(1,128)} %reshape.28.rows_ref, s32[40,512]{1,0:T(8,128)} %bitcast.12, s32[1,512]{1,0:T(1,128)} %bitcast.15), custom_call_target="tpu_custom_call" | custom-call | tf_op jit(solution)/shard_map/exchange_indices/pallas_call | solution.py:56
  30.7 1.4 copy.17
  32.1 95.2 %partials.1 = bf16[16,512,512]{2,1,0:T(8,128)(2,1)} custom-call(s32[16,640]{1,0:T(8,128)} %bitcast.13, s32[16,24,512]{2,1,0:T(8,128)} %get-tuple-element.7.aux_ref, bf16[8192,512]{1,0:T(8,128)(2,1)} %table_ref.1, bf16[512,512]{1,0:T(8,128)(2,1)} %wm_ref.1, bf16[512,512]{1,0:T(8,128)(2,1)} %ws_ref.1, bf16[512,512]{1,0:T(8,128)(2,1)} %wn_ref.1, f32[1,512]{1,0:T(1,128)} %bitcast.17), custom_call_target="tpu_custom_call" | custom-call | flops 24000000000 | bytes 24000000 | tf_op jit(solution)/shard_map/partials/pallas_call | solution.py:165
  127.3 0.0 copy-start.2
  127.3 51.0 %reduce_partials.1.pre_ref = f32[512,512]{1,0:T(8,128)S(1)} custom-call(bf16[4,4,512,512]{3,2,1,0:T(8,128)(2,1)} %bitcast.11), custom_call_target="tpu_custom_call" | custom-call | tf_op jit(solution)/shard_map/reduce_partials/pallas_call | solution.py:281
  178.3 0.0 all-gather.2.cloned.1.call-done.queries_ref
  178.4 0.0 copy-done.2
  178.4 0.0 copy-start
  178.4 3.4 %copy-done = bf16[8192,512]{1,0:T(8,128)(2,1)S(1)} copy-done((bf16[8192,512]{1,0:T(8,128)(2,1)S(1)}, bf16[8192,512]{1,0:T(8,128)(2,1)}, u32[]{:S(2)}) %copy-start) | copy-done | bytes 8388632
  181.7 8.9 %score.1 = (bf16[512,512]{1,0:T(8,128)(2,1)}, f32[8,2,1024]{2,1,0:T(2,128)S(1)}) custom-call(f32[512,512]{1,0:T(8,128)S(1)} %reduce_partials.1.pre_ref, f32[1,512]{1,0:T(1,128)S(1)} %bitcast.10, f32[512,1]{1,0:T(8,128)S(1)} %copy.14.logc_ref, bf16[8192,512]{1,0:T(8,128)(2,1)S(1)} %copy-done), custom_call_target="tpu_custom_call" | custom-call | tf_op jit(solution)/shard_map/score/pallas_call | solution.py:323
  190.6 0.0 copy-start.1
  190.6 0.6 copy-done.1
  191.2 20.0 %combine.1 = f32[1,1024]{1,0:T(1,128)} custom-call(f32[8,2,1024]{2,1,0:T(2,128)} %copy-done.1), custom_call_target="tpu_custom_call" | custom-call | tf_op jit(solution)/shard_map/combine/pallas_call | solution.py:380
  211.2 1.3 copy.19
Async XLA Ops:
  7.2 171.2 %all-gather.2.cloned.1.call-start = ((), (), s32[]{:S(2)}) async-start(), calls=%async_computation | async-start | bytes 9437184 | tf_op jit(solution)/shard_map/all_gather | solution.py:413
  127.3 51.1 %copy-start.2 = (f32[512]{0:T(512)S(1)}, f32[512]{0:T(512)}, u32[]{:S(2)}) copy-start(f32[512]{0:T(512)} %param.22) | copy-start | bytes 6148
  178.4 3.4 %copy-start = (bf16[8192,512]{1,0:T(8,128)(2,1)S(1)}, bf16[8192,512]{1,0:T(8,128)(2,1)}, u32[]{:S(2)}) copy-start(bf16[8192,512]{1,0:T(8,128)(2,1)} %all-gather.2.cloned.1.call-done.queries_ref) | copy-start | bytes 25165828
  190.6 0.6 copy-start.1
Sparse Core Ops, SparseCore 0:
  9.7 53.4 all-gather.1

commit v2 on v0

v2 whole, which is shorter than its diff:
```python
import functools
import math

import jax
import jax.numpy as jnp
from jax import lax
from jax.experimental import pallas as pl
from jax.experimental.pallas import tpu as pltpu
from jax.sharding import PartitionSpec as P

MESH = pl.DeviceIdType.MESH
VMEM = pl.BlockSpec(memory_space=pltpu.VMEM)


def greet(peers):
    barrier = pltpu.get_barrier_semaphore()
    for peer in peers:
        pl.semaphore_signal(barrier, inc=1, device_id=peer, device_id_type=MESH)
    pl.semaphore_wait(barrier, len(peers))


def remote(src, dst, send, recv, peer):
    return pltpu.make_async_remote_copy(
        src_ref=src, dst_ref=dst, send_sem=send, recv_sem=recv, device_id=peer, device_id_type=MESH
    )


def build_table(table_ref, wm_ref, ws_ref, wn_ref, bm_ref, t_ref, tbuf, in_sem):
    blk = 512
    blocks = 16

    def fetch(i, slot):
        return pltpu.make_async_copy(table_ref.at[pl.ds(i * blk, blk), :], tbuf.at[slot], in_sem.at[slot])

    fetch(0, 0).start()

    def build(i, _):
        slot = lax.rem(i, 2)

        @pl.when(i + 1 < blocks)
        def _():
            fetch(i + 1, 1 - slot).start()
        fetch(i, slot).wait()
        x = tbuf[slot]
        m = jnp.dot(x, wm_ref[...], preferred_element_type=jnp.float32) + bm_ref[...]
        m = jnp.maximum(m, 0.0).astype(jnp.bfloat16)
        t1 = jnp.dot(m, wn_ref[...], preferred_element_type=jnp.float32)
        t2 = jnp.dot(x, ws_ref[...], preferred_element_type=jnp.float32)
        base = pl.multiple_of(i * (blk * 8), 8)
        flat = t_ref.reshape(65536, 128)
        for j in range(4):
            flat[pl.ds(base + j, blk, stride=8), :] = t1[:, j * 128:(j + 1) * 128]
            flat[pl.ds(base + 4 + j, blk, stride=8), :] = t2[:, j * 128:(j + 1) * 128]
        return 0
    lax.fori_loop(0, blocks, build, 0)


GROUPS = ((0, 7), (7, 14), (14, 21), (21, 28), (28, 34), (34, 40))


def prepare(n, p, rows_ref, aux_ref, t_ref, g_ref, self_ref, rcnt_ref, key_ref, val_ref, gb_ref, c_ref, rc_ref):
    packed = aux_ref[n]
    for h, slots in enumerate((packed & 0xFFFF, lax.shift_right_logical(packed, 16))):
        rel = slots - 640 * p
        ok = (rel >= 0) & (rel < 640)
        key_ref[h * 24:(h + 1) * 24, :] = rel & 63
        shift = 3 * jnp.where(ok, lax.shift_right_logical(rel, 6), 0)
        val_ref[h * 24:(h + 1) * 24, :] = jnp.where(ok, jnp.left_shift(1, shift), 0)
    sub = lax.broadcasted_iota(jnp.int32, (64, 128), 0)
    lane = lax.broadcasted_iota(jnp.int32, (128, 128), 1)
    here = lane == n
    even = 0o0707070707
    for vb in range(4):
        for s in range(vb * 160, vb * 160 + 160):
            r = rows_ref[n * 640 + s]
            g_ref[s * 8:s * 8 + 8, :] = t_ref[r]
        cols = slice(vb * 128, (vb + 1) * 128)
        low = jnp.zeros((64, 128), jnp.int32)
        high = jnp.zeros((64, 128), jnp.int32)
        for first, last in GROUPS:
            acc = jnp.zeros((64, 128), jnp.int32)
            for k in range(first, last):
                kk = k if k < 20 else k + 4
                key = jnp.broadcast_to(key_ref[kk:kk + 1, cols], (64, 128))
                val = jnp.broadcast_to(val_ref[kk:kk + 1, cols], (64, 128))
                acc = acc + jnp.where(sub == key, val, 0)
            low = low + (acc & even)
            high = high + (lax.shift_right_logical(acc, 3) & even)
        ct = jnp.concatenate([low, high], axis=0).T
        self_col = jnp.sum(jnp.where(here, self_ref[cols, :], 0.0), axis=1, keepdims=True).astype(jnp.int32) - 640 * p
        rc_ref[cols, :] = jnp.sum(jnp.where(here, rcnt_ref[cols, :], 0.0), axis=1, keepdims=True)
        for f in range(5):
            c_ref[cols, f * 128:(f + 1) * 128] = (lax.shift_right_logical(ct, 6 * f) & 63).astype(jnp.float32).astype(jnp.bfloat16)
            c_ref[cols, 640 + f * 128:640 + (f + 1) * 128] = jnp.where(self_col == lane + f * 128, 1.0, 0.0).astype(jnp.bfloat16)
        for j in range(8):
            gb_ref[vb * 160:vb * 160 + 160, j * 128:(j + 1) * 128] = g_ref[pl.ds(vb * 1280 + j, 160, stride=8), :].astype(jnp.bfloat16)


def multiply(gb_ref, c_ref, rc_ref):
    part = jnp.dot(c_ref[:, :640], gb_ref[:, :512], preferred_element_type=jnp.float32) * rc_ref[...]
    part = part + jnp.dot(c_ref[:, 640:], gb_ref[:, 512:], preferred_element_type=jnp.float32)
    return part.astype(jnp.bfloat16)


ORDER = ((2, 2), (2, 1), (1, 2), (2, 3), (3, 2), (2, 0), (0, 2), (1, 1),
         (3, 3), (1, 3), (3, 1), (1, 0), (0, 1), (3, 0), (0, 3), (0, 0))
PLACE = {pair: i for i, pair in enumerate(ORDER)}
CODE = tuple(sum(pair[axis] * 4 ** i for i, pair in enumerate(ORDER)) for axis in range(2))


def tower_kernel(fetch_ref, slots_ref, count_ref, slot_ref, table_ref, wm_ref, ws_ref, wn_ref, bm_ref, queries_ref,
                 pre_ref, all_ref,
                 t_ref, tbuf, g_ref, gb0, gb1, c0, c1, rc0, rc1, key_ref, val_ref, self_ref, rcnt_ref, p_ref,
                 rows_own, rows_got, rows_sm, aux_own, aux, near, far, near2, far2,
                 in_sem, row_send, row_recv, aux_send, aux_recv, sm_sem, own_sem, q_send, q_recv,
                 send1, recv1, send2, recv2):
    me = lax.axis_index("neg")
    q = lax.axis_index("qry")
    spot = (me // 4, lax.rem(me, 4))
    peers = [{"neg": lax.rem(me + d, 16)} for d in range(1, 16)]
    above, below = lax.rem(q + 2, 8), lax.rem(q + 6, 8)
    partner = q + 1 - 2 * lax.rem(q, 2)
    across = lax.rem(q + 4, 8)

    def device(axis, step):
        moved = lax.rem(spot[axis] + step + 4, 4)
        return {"neg": moved * 4 + spot[1] if axis == 0 else spot[0] * 4 + moved}

    for j in range(16):
        rows_own[j] = fetch_ref[j:j + 1, :]
    count = count_ref[...]
    for h in range(2):
        ks = lax.broadcasted_iota(jnp.int32, (20, 512), 0) + 20 * h
        half = jnp.where(ks < count, slots_ref[20 * h:20 * h + 20, :], 0xFFFF)
        if h == 0:
            low = half
        else:
            aux_own[0:20, :] = low | jnp.left_shift(half, 16)
    aux_own[20:24, :] = jnp.broadcast_to(slot_ref[...] | jnp.left_shift(count, 16), (4, 512))

    greet(peers + [{"qry": above}, {"qry": below}, {"qry": partner}])
    row_copies = []
    aux_copies = []
    for d, peer in enumerate(peers):
        other = lax.rem(me + d + 1, 16)
        row_copies.append(remote(rows_own.at[other], rows_got.at[me], row_send.at[d], row_recv.at[d], peer))
    for d, peer in enumerate(peers):
        aux_copies.append(remote(aux_own, aux.at[me], aux_send.at[d], aux_recv.at[d], peer))
    for copy in row_copies + aux_copies:
        copy.start()
    rows_got[me] = rows_own[me]
    aux[me] = aux_own[...]

    def pass_on(i, source, place, size, peer):
        return remote(source, all_ref.at[pl.ds(place, size), :], q_send.at[i], q_recv.at[i], {"qry": peer})

    own_copy = pltpu.make_async_copy(queries_ref, all_ref.at[pl.ds(q * 1024, 1024), :], own_sem)
    spread = [pass_on(i, queries_ref, q * 1024, 1024, peer) for i, peer in enumerate((above, below, partner))]

    def held(i, place, size, peer):
        return pass_on(i, all_ref.at[pl.ds(place, size), :], place, size, peer)

    relay = [
        held(3, below * 1024, 512, above),
        held(4, above * 1024 + 512, 512, below),
        held(5, below * 1024, 1024, partner),
        held(6, above * 1024, 1024, partner),
    ]
    hand = [held(7, across * 1024, 512, partner), held(8, across * 1024 + 512, 512, partner)]
    own_copy.start()
    for copy in spread:
        copy.start()

    build_table(table_ref, wm_ref, ws_ref, wn_ref, bm_ref, t_ref, tbuf, in_sem)

    for copy in row_copies:
        copy.wait_recv()
    to_scalar = [
        pltpu.make_async_copy(rows_got.at[j, 0], rows_sm.at[pl.ds(j * 640, 640)], sm_sem.at[j]) for j in range(16)
    ]
    for copy in to_scalar:
        copy.start()
    for copy in aux_copies:
        copy.wait_recv()
    last = aux[:, 20, :]
    last = jnp.concatenate([last] * 8, axis=0)
    self_ref[...] = (last & 0xFFFF).astype(jnp.float32).T
    rcnt_ref[...] = (1.0 / lax.shift_right_logical(last, 16).astype(jnp.float32)).T
    for copy in to_scalar:
        copy.wait()

    def near_copy(half, w, j):
        pair = (2, j) if half == 0 else (j, 2)
        rows = pl.ds(256 * half + 128 * w, 128)
        return remote(p_ref.at[PLACE[pair], rows, :], near.at[half, w, j],
                      send1.at[half, w, 0, j], recv1.at[half, w, 0, j], device(half, 1 - 2 * w))

    def far_copy(half, w, stage, j):
        side = 1 + 2 * w
        pair = (side, j) if half == 0 else (j, side)
        part = w if stage == 2 else 1 - w
        rows = pl.ds(256 * half + 128 * part, 128)
        return remote(p_ref.at[PLACE[pair], rows, :], far.at[half, w, 2 - stage, j],
                      send1.at[half, w, stage, j], recv1.at[half, w, stage, j], device(half, 1 - 2 * w))

    def send_place(c):
        for half in range(2):
            d, j = ORDER[c][half], ORDER[c][1 - half]
            if d == 2:
                for w in range(2):
                    near_copy(half, w, j).start()
            elif d != 0:
                far_copy(half, (d - 1) // 2, 1, j).start()

    def step(dx, dy, gb, c, rc):
        n = lax.rem(spot[0] + dx, 4) * 4 + lax.rem(spot[1] + dy, 4)
        prepare(n, me, rows_sm, aux, t_ref, g_ref, self_ref, rcnt_ref, key_ref, val_ref, gb, c, rc)

    step(ORDER[0][0], ORDER[0][1], gb0, c0, rc0)

    def two(i, codes):
        cx, cy = codes
        step(lax.rem(cx, 4), lax.rem(cy, 4), gb1, c1, rc1)
        p_ref[2 * i] = multiply(gb0, c0, rc0)
        for place in range(8):
            @pl.when(i == place)
            def _():
                send_place(2 * place)
        cx, cy = cx // 4, cy // 4
        step(lax.rem(cx, 4), lax.rem(cy, 4), gb0, c0, rc0)
        p_ref[2 * i + 1] = multiply(gb1, c1, rc1)
        for place in range(8):
            @pl.when(i == place)
            def _():
                send_place(2 * place + 1)
        return cx // 4, cy // 4
    lax.fori_loop(0, 8, two, (jnp.int32(CODE[0] // 4), jnp.int32(CODE[1] // 4)))

    f32 = jnp.float32
    for copy in spread:
        copy.wait_recv()
    for copy in relay:
        copy.start()

    for j in (2, 1, 3, 0):
        for half in range(2):
            for w in range(2):
                near_copy(half, w, j).wait_recv()
                side = 1 + 2 * w
                pair = (side, j) if half == 0 else (j, side)
                rows = slice(256 * half + 128 * w, 256 * half + 128 * w + 128)
                value = p_ref[PLACE[pair], rows, :].astype(f32) + near[half, w, j].astype(f32)
                p_ref[PLACE[pair], rows, :] = value.astype(jnp.bfloat16)
                far_copy(half, w, 2, j).start()

    def home_at(half, j, part):
        first = 256 * half + 128 * part
        return PLACE[(0, j) if half == 0 else (j, 0)], slice(first, first + 128), slice(None)

    def second_copy(half, w, stage):
        target = (near2.at[half, w], far2.at[half, w, 1], far2.at[half, w, 0])[stage]
        return remote(p_ref.at[home_at(half, (2, 1 + 2 * w, 1 + 2 * w)[stage], (w, 1 - w, w)[stage])], target, send2.at[half, w, stage], recv2.at[half, w, stage],
                      device(1 - half, 1 - 2 * w))

    def total_at(half, j, part, c):
        first = (((half * 4 + j) * 2 + part) * 4 + c) * 16
        return slice(first, first + 16), slice(None), slice(None)

    for j in (2, 1, 3, 0):
        for half in range(2):
            for part in range(2):
                far_copy(half, part, 2, j).wait_recv()
                far_copy(half, part, 1, j).wait_recv()
        for half in range(2):
            for part in range(2):
                value = p_ref[home_at(half, j, part)].astype(f32) + far[half, part, 0, j].astype(f32)
                value = value + far[half, 1 - part, 1, j].astype(f32)
                if j == 2:
                    p_ref[home_at(half, j, part)] = value.astype(jnp.bfloat16)
                    second_copy(half, part, 0).start()
                    continue
                if j != 0 and part == 1 - (j - 1) // 2:
                    p_ref[home_at(half, j, part)] = value.astype(jnp.bfloat16)
                    second_copy(half, 1 - part, 1).start()
                    continue
                for c in range(4):
                    t_ref[total_at(half, j, part, c)] = value[:, c * 128:(c + 1) * 128].reshape(16, 8, 128)
    for half in range(2):
        for w in range(2):
            second_copy(half, w, 0).wait_recv()
            for c in range(4):
                lanes = slice(c * 128, (c + 1) * 128)
                value = t_ref[total_at(half, 1 + 2 * w, w, c)].reshape(128, 128) + near2[half, w, :, lanes].astype(f32)
                place, rows, _ = home_at(half, 1 + 2 * w, w)
                p_ref[place, rows, lanes] = value.astype(jnp.bfloat16)
            second_copy(half, w, 2).start()
    for copy in relay:
        copy.wait_recv()
    for copy in hand:
        copy.start()
    for half in range(2):
        for w in range(2):
            second_copy(half, w, 1).wait_recv()
            second_copy(half, w, 2).wait_recv()
        for w in range(2):
            rows = slice(256 * half + 128 * w, 256 * half + 128 * w + 128)
            for c in range(4):
                lanes = slice(c * 128, (c + 1) * 128)
                value = t_ref[total_at(half, 0, w, c)].reshape(128, 128) + far2[half, w, 0, :, lanes].astype(f32)
                pre_ref[rows, lanes] = value + far2[half, 1 - w, 1, :, lanes].astype(f32)
    own_copy.wait()
    for copy in hand:
        copy.wait_recv()
    for copy in row_copies + aux_copies + spread + relay + hand:
        copy.wait_send()
    for half in range(2):
        for w in range(2):
            for j in range(4):
                near_copy(half, w, j).wait_send()
                far_copy(half, w, 1, j).wait_send()
                far_copy(half, w, 2, j).wait_send()
            for stage in range(3):
                second_copy(half, w, stage).wait_send()


def tower(fetch_rows, slots, count, slot, table, wm, ws, wn, bm, queries):
    any_space = pl.BlockSpec(memory_space=pl.ANY)
    bf16, f32, i32 = jnp.bfloat16, jnp.float32, jnp.int32
    dma = pltpu.SemaphoreType.DMA
    return pl.pallas_call(
        tower_kernel,
        out_shape=(
            jax.ShapeDtypeStruct((512, 512), f32),
            jax.ShapeDtypeStruct((8192, 512), bf16),
        ),
        in_specs=[VMEM] * 4 + [any_space] + [VMEM] * 4 + [any_space],
        out_specs=(VMEM, any_space),
        scratch_shapes=[
            pltpu.VMEM((8192, 8, 128), f32),
            pltpu.VMEM((2, 512, 512), bf16),
            pltpu.VMEM((5120, 128), f32),
            pltpu.VMEM((640, 1024), bf16),
            pltpu.VMEM((640, 1024), bf16),
            pltpu.VMEM((512, 1280), bf16),
            pltpu.VMEM((512, 1280), bf16),
            pltpu.VMEM((512, 1), f32),
            pltpu.VMEM((512, 1), f32),
            pltpu.VMEM((48, 512), i32),
            pltpu.VMEM((48, 512), i32),
            pltpu.VMEM((512, 128), f32),
            pltpu.VMEM((512, 128), f32),
            pltpu.VMEM((16, 512, 512), bf16),
            pltpu.VMEM((16, 1, 640), i32),
            pltpu.VMEM((16, 1, 640), i32),
            pltpu.SMEM((10240,), i32),
            pltpu.VMEM((24, 512), i32),
            pltpu.VMEM((16, 24, 512), i32),
            pltpu.VMEM((2, 2, 4, 128, 512), bf16),
            pltpu.VMEM((2, 2, 2, 4, 128, 512), bf16),
            pltpu.VMEM((2, 2, 128, 512), bf16),
            pltpu.VMEM((2, 2, 2, 128, 512), bf16),
            dma((2,)),
            dma((15,)), dma((15,)), dma((15,)), dma((15,)),
            dma((16,)), dma, dma((9,)), dma((9,)),
            dma((2, 2, 3, 4)), dma((2, 2, 3, 4)), dma((2, 2, 3)), dma((2, 2, 3)),
        ],
        compiler_params=pltpu.CompilerParams(
            collective_id=1, has_side_effects=True, vmem_limit_bytes=67043328),
        name="tower",
    )(fetch_rows, slots, count, slot, table, wm, ws, wn, bm, queries)


def joined(stats):
    peak = jnp.max(stats[:, 0:1, :], axis=0)
    total = jnp.sum(stats[:, 1:2, :] * jnp.exp(stats[:, 0:1, :] - peak[None]), axis=0)
    return peak, total


def score_kernel(pre_ref, bias_ref, logc_ref, queries_ref, embed_ref, lse_ref,
                 scaled, qbuf, stats, got, mine, final, in_sem, send_sem, recv_sem, send_sem2, recv_sem2):
    q = lax.axis_index("qry")
    n = lax.axis_index("neg")
    row_peers = [{"qry": lax.rem(q + d, 8)} for d in range(1, 8)]
    column_peers = [{"neg": lax.rem(n + d, 16)} for d in range(1, 16)]

    def fetch(d):
        block = lax.rem(q + d, 8)
        return pltpu.make_async_copy(queries_ref.at[pl.ds(block * 1024, 1024), :], qbuf.at[d - 1], in_sem.at[d - 1])

    for d in range(1, 9):
        fetch(d).start()
    hidden = jnp.maximum(pre_ref[...] + bias_ref[...], 0.0)
    inv = lax.rsqrt(jnp.mean(hidden * hidden, axis=-1, keepdims=True) + 0.25)
    embed = (hidden * inv).astype(jnp.bfloat16)
    embed_ref[...] = embed
    scaled[...] = embed * jnp.bfloat16(0.25)
    greet(row_peers + column_peers)

    def block_copy(i, d):
        return remote(stats.at[i], got.at[q], send_sem.at[d - 1], recv_sem.at[d - 1], {"qry": lax.rem(q + d, 8)})

    def block(i, _):
        pltpu.make_async_copy(queries_ref.at[pl.ds(lax.rem(q + i + 1, 8) * 1024, 1024), :], qbuf.at[i], in_sem.at[i]).wait()
        for part in range(2):
            cols = pl.ds(part * 512, 512)
            scores = lax.dot_general(
                scaled[...], qbuf[i, cols, :], (((1,), (1,)), ((), ())), preferred_element_type=jnp.float32
            ) - logc_ref[...]
            peak = jnp.max(scores, axis=0, keepdims=True)
            total = jnp.sum(jnp.exp(scores - peak), axis=0, keepdims=True)
            stats[i, 0:1, cols] = peak
            stats[i, 1:2, cols] = total
        for d in range(1, 8):
            @pl.when(i == d - 1)
            def _():
                block_copy(d - 1, d).start()
        return 0
    lax.fori_loop(0, 8, block, 0)
    got[q] = stats[7]
    copies = [block_copy(d - 1, d) for d in range(1, 8)]
    for copy in copies:
        copy.wait_recv()
    peak, total = joined(got[...])
    mine[...] = jnp.concatenate([peak, total], axis=0)
    final[n] = mine[...]
    for d, peer in enumerate(column_peers):
        copies.append(remote(mine, final.at[n], send_sem2.at[d], recv_sem2.at[d], peer))
        copies[-1].start()
    for copy in copies[7:]:
        copy.wait_recv()
    peak, total = joined(final[...])
    lse_ref[...] = peak + jnp.log(total) - math.log(65536)
    for copy in copies:
        copy.wait_send()


def score(pre, bias, log_count, queries):
    f32 = jnp.float32
    dma = pltpu.SemaphoreType.DMA
    return pl.pallas_call(
        score_kernel,
        out_shape=(
            jax.ShapeDtypeStruct((512, 512), jnp.bfloat16),
            jax.ShapeDtypeStruct((1, 1024), f32),
        ),
        in_specs=[VMEM, VMEM, VMEM, pl.BlockSpec(memory_space=pl.ANY)],
        out_specs=(VMEM, VMEM),
        scratch_shapes=[
            pltpu.VMEM((512, 512), jnp.bfloat16),
            pltpu.VMEM((8, 1024, 512), jnp.bfloat16),
            pltpu.VMEM((8, 2, 1024), f32),
            pltpu.VMEM((8, 2, 1024), f32),
            pltpu.VMEM((2, 1024), f32),
            pltpu.VMEM((16, 2, 1024), f32),
            dma((8,)), dma((7,)), dma((7,)), dma((15,)), dma((15,)),
        ],
        compiler_params=pltpu.CompilerParams(
            collective_id=2, has_side_effects=True, vmem_limit_bytes=48 * 1024 * 1024),
        name="score",
    )(pre, bias, log_count, queries)


def per_device(
    items_table,
    fetch_rows,
    neighbour_slots,
    neighbour_count,
    self_slot,
    negative_count,
    message_weight,
    message_bias,
    self_weight,
    neighbour_weight,
    output_bias,
    queries,
):
    own_count = lax.dynamic_slice(negative_count, (lax.axis_index("qry") * 512,), (512,))
    log_count = jnp.log(own_count.astype(jnp.float32)).reshape(512, 1)
    pre, queries_all = tower(
        fetch_rows, neighbour_slots.T, neighbour_count.reshape(1, 512), self_slot.reshape(1, 512), items_table,
        message_weight, self_weight, neighbour_weight, message_bias.reshape(1, 512), queries)
    negative_embed, query_lse = score(pre, output_bias.reshape(1, 512), log_count, queries_all)
    return negative_embed, query_lse.reshape(1024)


def solution(mesh):
    in_specs = (
        P("neg", None),
        P(("neg", "qry"), None),
        P(("neg", "qry"), None),
        P(("neg", "qry")),
        P(("neg", "qry")),
        P("neg"),
        P(),
        P(),
        P(),
        P(),
        P(),
        P("qry", None),
    )
    out_specs = (P(("neg", "qry"), None), P("qry"))
    return jax.shard_map(
        per_device, mesh=mesh, in_specs=in_specs, out_specs=out_specs, check_vma=False
    )
```

time: 451 us -> 129 us (0.29)
  waiting for transfers between devices: 221 us -> 0 us
  local copies, waits for them, and re-layouts: 146 us -> 5.1 us
  Pallas kernels: 0 us -> 122 us
  other arithmetic: 23.1 us -> 0.77 us
  matrix products: 20.3 us -> 0 us
  blocking collectives: 13.9 us -> 0 us
  between operations: 14.3 us -> 0.66 us
  starting transfers between devices: 11.6 us -> 0 us
    all_to_all x2 -> x0, waiting for transfers between devices: 180 us -> none  [the longest x1 174 us: per_device(): lax.all_to_all(served, 'neg', split_axis=0, concat_axis=0, tiled=True)]
    gather x3 -> x0, local copies, waits for them, and re-layouts: 143 us -> none  [the longest x1 88.5 us: per_device(): gathered = message[neighbour_slots]]
    pallas_call x0 -> x2, Pallas kernels: none -> 122 us  [the longest x1 102 us: tower(): pl.pallas_call(tower_kernel, out_shape=(jax.ShapeDtypeStruct((512, 512),...]
    all_gather x1 -> x0, waiting for transfers between devices: 41.5 us -> none  [per_device(): lax.all_gather(negative_embed, 'qry', axis=0, tiled=True)]
    reduce_sum x2 -> x0, other arithmetic: 21.2 us -> none  [the longest x1 17.6 us: per_device(): jnp.sum(jnp.where(live_mask[:, :, None], gathered, jnp.zeros((), jnp.bflo...]
    dot_general x4 -> x0, matrix products: 20.3 us -> none  [the longest x1 10.8 us: make_message(): jnp.dot(rows, message_weight, preferred_element_type=jnp.float32)]
    all_to_all x1 -> x0, blocking collectives: 13.9 us -> none  [per_device(): lax.all_to_all(fetch_rows, 'neg', split_axis=0, concat_axis=0, tiled=True)]
    all_to_all x2 -> x0, starting transfers between devices: 11.5 us -> none  [the longest x1 6.53 us: from_everyone(): lax.all_to_all(jnp.broadcast_to(x[None], (devices, *x.shape)), axis, 0, 0...]
  transfers between devices with their start and end apart: 3 -> 0, of which waited for: 3 -> 0; matrix products, arithmetic and copies ran while one was open for 0% -> 0% of each run, Pallas kernels for 0% -> 0%
where the time goes in v2:
time: 129 us
  Pallas kernels  122 us (95%)
  local copies, waits for them, and re-layouts  5.1 us (4%)
    pallas_call x1, Pallas kernels, tower(): pl.pallas_call(tower_kernel, out_shape=(jax.ShapeDtypeStruct((512, 512),...  102 us
    pallas_call x1, Pallas kernels, score(): pl.pallas_call(score_kernel, out_shape=(jax.ShapeDtypeStruct((512, 512),...  20.6 us
    unnamed x8, local copies, waits for them, and re-layouts  4.24 us

profile of v2, /device:TPU:1, one launch (start us, length us, event | category | flops | bytes accessed | tf_op | source)
XLA Modules:
  0.0 128.9 jit_solution(3694773092023753623)
XLA Ops:
  0.6 0.8 convert_log_fusion
  1.4 0.9 copy.14.logc_ref
  2.3 101.8 %tower.1 = (f32[512,512]{1,0:T(8,128)}, bf16[8192,512]{1,0:T(8,128)(2,1)}) custom-call(s32[16,640]{1,0:T(8,128)} %fetch_ref.1, s32[40,512]{1,0:T(8,128)} %bitcast.9, s32[1,512]{1,0:T(1,128)} %bitcast.11, s32[1,512]{1,0:T(1,128)} %bitcast.12, bf16[8192,512]{1,0:T(8,128)(2,1)} %table_ref.1, bf16[512,512]{1,0:T(8,128)(2,1)} %wm_ref.1, bf16[512,512]{1,0:T(8,128)(2,1)} %ws_ref.1, ...), custom_call_target="tpu_custom_call" | custom-call | tf_op jit(solution)/shard_map/tower/pallas_call | solution.py:330
  104.1 0.0 copy-start
  104.1 1.2 copy-done
  105.3 0.0 copy-start.1
  105.3 0.9 copy-done.1
  106.2 0.0 copy-start.2
  106.2 0.7 copy-done.2
  106.9 20.6 %score.1 = (bf16[512,512]{1,0:T(8,128)(2,1)S(1)}, f32[1,1024]{1,0:T(1,128)S(1)}) custom-call(f32[512,512]{1,0:T(8,128)S(1)} %copy-done, f32[1,512]{1,0:T(1,128)S(1)} %bitcast.8, f32[512,1]{1,0:T(8,128)S(1)} %copy-done.1, bf16[8192,512]{1,0:T(8,128)(2,1)} %get-tuple-element.7.queries_ref), custom_call_target="tpu_custom_call" | custom-call | tf_op jit(solution)/shard_map/score/pallas_call | solution.py:440
  127.6 0.8 copy.17
  128.3 0.6 copy.18
Async XLA Ops:
  104.1 1.2 copy-start
  105.3 0.9 copy-start.1
  106.2 0.7 copy-start.2

commit v3 on v2

v3 whole, which is shorter than its diff:
```python
import functools
import math

import jax
import jax.numpy as jnp
from jax import lax
from jax.experimental import pallas as pl
from jax.experimental.pallas import tpu as pltpu
from jax.sharding import PartitionSpec as P

MESH = pl.DeviceIdType.MESH
VMEM = pl.BlockSpec(memory_space=pltpu.VMEM)


def greet(peers):
    barrier = pltpu.get_barrier_semaphore()
    for peer in peers:
        pl.semaphore_signal(barrier, inc=1, device_id=peer, device_id_type=MESH)
    pl.semaphore_wait(barrier, len(peers))


def remote(src, dst, send, recv, peer):
    return pltpu.make_async_remote_copy(
        src_ref=src, dst_ref=dst, send_sem=send, recv_sem=recv, device_id=peer, device_id_type=MESH
    )


def build_table(table_ref, wm_ref, ws_ref, wn_ref, bm_ref, t_ref, tbuf, in_sem):
    blk = 512
    blocks = 16

    def fetch(i, slot):
        return pltpu.make_async_copy(table_ref.at[pl.ds(i * blk, blk), :], tbuf.at[slot], in_sem.at[slot])

    fetch(0, 0).start()

    def build(i, _):
        slot = lax.rem(i, 2)

        @pl.when(i + 1 < blocks)
        def _():
            fetch(i + 1, 1 - slot).start()
        fetch(i, slot).wait()
        x = tbuf[slot]
        m = jnp.dot(x, wm_ref[...], preferred_element_type=jnp.float32) + bm_ref[...]
        m = jnp.maximum(m, 0.0).astype(jnp.bfloat16)
        t1 = jnp.dot(m, wn_ref[...], preferred_element_type=jnp.float32)
        t2 = jnp.dot(x, ws_ref[...], preferred_element_type=jnp.float32)
        base = pl.multiple_of(i * (blk * 8), 8)
        flat = t_ref.reshape(65536, 128)
        for j in range(4):
            flat[pl.ds(base + j, blk, stride=8), :] = t1[:, j * 128:(j + 1) * 128]
            flat[pl.ds(base + 4 + j, blk, stride=8), :] = t2[:, j * 128:(j + 1) * 128]
        return 0
    lax.fori_loop(0, blocks, build, 0)


GROUPS = ((0, 7), (7, 14), (14, 21), (21, 28), (28, 34), (34, 40))


def prepare(n, p, rows_ref, aux_ref, t_ref, g_ref, self_ref, rcnt_ref, key_ref, val_ref, gb_ref, c_ref, rc_ref):
    packed = aux_ref[n]
    for h, slots in enumerate((packed & 0xFFFF, lax.shift_right_logical(packed, 16))):
        rel = slots - 640 * p
        ok = (rel >= 0) & (rel < 640)
        key_ref[h * 24:(h + 1) * 24, :] = rel & 63
        shift = 3 * jnp.where(ok, lax.shift_right_logical(rel, 6), 0)
        val_ref[h * 24:(h + 1) * 24, :] = jnp.where(ok, jnp.left_shift(1, shift), 0)
    sub = lax.broadcasted_iota(jnp.int32, (64, 128), 0)
    lane = lax.broadcasted_iota(jnp.int32, (128, 128), 1)
    here = lane == n
    even = 0o0707070707
    for vb in range(4):
        for s in range(vb * 160, vb * 160 + 160):
            r = rows_ref[n * 640 + s]
            g_ref[s * 8:s * 8 + 8, :] = t_ref[r]
        cols = slice(vb * 128, (vb + 1) * 128)
        low = jnp.zeros((64, 128), jnp.int32)
        high = jnp.zeros((64, 128), jnp.int32)
        for first, last in GROUPS:
            acc = jnp.zeros((64, 128), jnp.int32)
            for k in range(first, last):
                kk = k if k < 20 else k + 4
                key = jnp.broadcast_to(key_ref[kk:kk + 1, cols], (64, 128))
                val = jnp.broadcast_to(val_ref[kk:kk + 1, cols], (64, 128))
                acc = acc + jnp.where(sub == key, val, 0)
            low = low + (acc & even)
            high = high + (lax.shift_right_logical(acc, 3) & even)
        ct = jnp.concatenate([low, high], axis=0).T
        self_col = jnp.sum(jnp.where(here, self_ref[cols, :], 0.0), axis=1, keepdims=True).astype(jnp.int32) - 640 * p
        rc_ref[cols, :] = jnp.sum(jnp.where(here, rcnt_ref[cols, :], 0.0), axis=1, keepdims=True)
        for f in range(5):
            c_ref[cols, f * 128:(f + 1) * 128] = (lax.shift_right_logical(ct, 6 * f) & 63).astype(jnp.float32).astype(jnp.bfloat16)
            c_ref[cols, 640 + f * 128:640 + (f + 1) * 128] = jnp.where(self_col == lane + f * 128, 1.0, 0.0).astype(jnp.bfloat16)
        for j in range(8):
            gb_ref[vb * 160:vb * 160 + 160, j * 128:(j + 1) * 128] = g_ref[pl.ds(vb * 1280 + j, 160, stride=8), :].astype(jnp.bfloat16)


def multiply(gb_ref, c_ref, rc_ref):
    part = jnp.dot(c_ref[:, :640], gb_ref[:, :512], preferred_element_type=jnp.float32) * rc_ref[...]
    part = part + jnp.dot(c_ref[:, 640:], gb_ref[:, 512:], preferred_element_type=jnp.float32)
    return part.astype(jnp.bfloat16)


ORDER = ((2, 2), (1, 2), (3, 2), (2, 1), (2, 3), (1, 1), (3, 3), (2, 0),
         (0, 2), (1, 3), (3, 1), (1, 0), (0, 1), (3, 0), (0, 3), (0, 0))
PLACE = {pair: i for i, pair in enumerate(ORDER)}
CODE = tuple(sum(pair[axis] * 4 ** i for i, pair in enumerate(ORDER)) for axis in range(2))


CARRY_AT = {
    (0, 0, 2): 3, (0, 1, 2): 3, (1, 0, 2): 4, (1, 1, 2): 4, (0, 0, 1): 7, (0, 1, 1): 10, (0, 0, 3): 9, (0, 1, 3): 8,
    (1, 0, 1): 6, (1, 1, 1): 9, (1, 0, 3): 10, (1, 1, 3): 7, (0, 0, 0): 11, (0, 1, 0): 13, (1, 0, 0): 12, (1, 1, 0): 14,
}
HOME_AT = {(0, 2): 8, (1, 2): 9, (1, 1): 13, (0, 1): 14, (0, 3): 14, (1, 3): 14}
RELAY_AT, HAND_AT = 5, 12

def tower_kernel(fetch_ref, slots_ref, count_ref, slot_ref, table_ref, wm_ref, ws_ref, wn_ref, bm_ref, bias_ref,
                 sampled_ref, queries_ref,
                 embed_ref, lse_ref, all_ref,
                 t_ref, tbuf, g_ref, gb0, gb1, c0, c1, rc0, rc1, key_ref, val_ref, self_ref, rcnt_ref, p_ref,
                 rows_own, rows_got, rows_sm, aux_own, aux, mail, near2, far2, logc_ref, stats, got, mine, final,
                 in_sem, row_send, row_recv, aux_send, aux_recv, sm_sem, own_sem, q_send, q_recv,
                 send1, recv1, send2, recv2, load_sem, send3, recv3, send4, recv4):
    me = lax.axis_index("neg")
    q = lax.axis_index("qry")
    spot = (me // 4, lax.rem(me, 4))
    peers = [{"neg": lax.rem(me + d, 16)} for d in range(1, 16)]
    above, below = lax.rem(q + 2, 8), lax.rem(q + 6, 8)
    partner = q + 1 - 2 * lax.rem(q, 2)
    across = lax.rem(q + 4, 8)

    def device(axis, step):
        moved = lax.rem(spot[axis] + step + 4, 4)
        return {"neg": moved * 4 + spot[1] if axis == 0 else spot[0] * 4 + moved}

    for j in range(16):
        rows_own[j] = fetch_ref[j:j + 1, :]
    count = count_ref[...]
    for h in range(2):
        ks = lax.broadcasted_iota(jnp.int32, (20, 512), 0) + 20 * h
        half = jnp.where(ks < count, slots_ref[20 * h:20 * h + 20, :], 0xFFFF)
        if h == 0:
            low = half
        else:
            aux_own[0:20, :] = low | jnp.left_shift(half, 16)
    aux_own[20:24, :] = jnp.broadcast_to(slot_ref[...] | jnp.left_shift(count, 16), (4, 512))

    sampled = sampled_ref[:, pl.ds(pl.multiple_of(q * 512, 128), 512)].astype(jnp.float32)
    logc_ref[...] = jnp.broadcast_to(jnp.log(sampled), (128, 512)).T

    row_peers = [{"qry": lax.rem(q + d, 8)} for d in range(1, 8)]
    greet(peers + row_peers)
    row_copies = []
    aux_copies = []
    for d, peer in enumerate(peers):
        other = lax.rem(me + d + 1, 16)
        row_copies.append(remote(rows_own.at[other], rows_got.at[me], row_send.at[d], row_recv.at[d], peer))
    for d, peer in enumerate(peers):
        aux_copies.append(remote(aux_own, aux.at[me], aux_send.at[d], aux_recv.at[d], peer))
    for copy in row_copies + aux_copies:
        copy.start()
    rows_got[me] = rows_own[me]
    aux[me] = aux_own[...]

    def pass_on(i, source, place, size, peer):
        return remote(source, all_ref.at[pl.ds(place, size)], q_send.at[i], q_recv.at[i], {"qry": peer})

    own_copy = pltpu.make_async_copy(queries_ref, all_ref.at[pl.ds(q * 2, 2)], own_sem)
    spread = [pass_on(i, queries_ref, q * 2, 2, peer) for i, peer in enumerate((above, below, partner))]

    def held(i, place, size, peer):
        return pass_on(i, all_ref.at[pl.ds(place, size)], place, size, peer)

    relay = [
        held(3, below * 2, 1, above),
        held(4, above * 2 + 1, 1, below),
        held(5, below * 2, 2, partner),
        held(6, above * 2, 2, partner),
    ]
    hand = [held(7, across * 2, 1, partner), held(8, across * 2 + 1, 1, partner)]
    own_copy.start()
    for copy in spread:
        copy.start()

    build_table(table_ref, wm_ref, ws_ref, wn_ref, bm_ref, t_ref, tbuf, in_sem)

    for copy in row_copies:
        copy.wait_recv()
    to_scalar = [
        pltpu.make_async_copy(rows_got.at[j, 0], rows_sm.at[pl.ds(j * 640, 640)], sm_sem.at[j]) for j in range(16)
    ]
    for copy in to_scalar:
        copy.start()
    for copy in aux_copies:
        copy.wait_recv()
    last = aux[:, 20, :]
    last = jnp.concatenate([last] * 8, axis=0)
    self_ref[...] = (last & 0xFFFF).astype(jnp.float32).T
    rcnt_ref[...] = (1.0 / lax.shift_right_logical(last, 16).astype(jnp.float32)).T
    for copy in to_scalar:
        copy.wait()

    def near_copy(half, w, j):
        pair = (2, j) if half == 0 else (j, 2)
        rows = pl.ds(256 * half + 128 * w, 128)
        return remote(p_ref.at[PLACE[pair], rows, :], mail.at[half * 2 + w, j],
                      send1.at[half, w, 0, j], recv1.at[half, w, 0, j], device(half, 1 - 2 * w))

    def far_copy(half, w, stage, j):
        side = 1 + 2 * w
        pair = (side, j) if half == 0 else (j, side)
        part = w if stage == 2 else 1 - w
        rows = pl.ds(256 * half + 128 * part, 128)
        return remote(p_ref.at[PLACE[pair], rows, :], mail.at[4 + (half * 2 + w) * 2 + 2 - stage, j],
                      send1.at[half, w, stage, j], recv1.at[half, w, stage, j], device(half, 1 - 2 * w))

    def send_place(c):
        for half in range(2):
            d, j = ORDER[c][half], ORDER[c][1 - half]
            if d == 2:
                for w in range(2):
                    near_copy(half, w, j).start()
            elif d != 0:
                far_copy(half, (d - 1) // 2, 1, j).start()

    def step(dx, dy, gb, c, rc):
        n = lax.rem(spot[0] + dx, 4) * 4 + lax.rem(spot[1] + dy, 4)
        prepare(n, me, rows_sm, aux, t_ref, g_ref, self_ref, rcnt_ref, key_ref, val_ref, gb, c, rc)

    f32 = jnp.float32

    def carry(half, w, j):
        near_copy(half, w, j).wait_recv()
        side = 1 + 2 * w
        pair = (side, j) if half == 0 else (j, side)
        rows = slice(256 * half + 128 * w, 256 * half + 128 * w + 128)
        value = p_ref[PLACE[pair], rows, :].astype(f32) + mail[half * 2 + w, j].astype(f32)
        p_ref[PLACE[pair], rows, :] = value.astype(jnp.bfloat16)
        far_copy(half, w, 2, j).start()

    def home_at(half, j, part):
        first = 256 * half + 128 * part
        return PLACE[(0, j) if half == 0 else (j, 0)], slice(first, first + 128), slice(None)

    def second_copy(half, w, stage):
        target = (near2.at[half, w], far2.at[half, w, 1], far2.at[half, w, 0])[stage]
        place, rows, _ = home_at(half, (2, 1 + 2 * w, 1 + 2 * w)[stage], (w, 1 - w, w)[stage])
        return remote(p_ref.at[place, rows, :], target, send2.at[half, w, stage], recv2.at[half, w, stage],
                      device(1 - half, 1 - 2 * w))

    def arrive(half, j, part):
        far_copy(half, part, 2, j).wait_recv()
        far_copy(half, 1 - part, 1, j).wait_recv()

    def total(half, j, part):
        value = p_ref[home_at(half, j, part)].astype(f32) + mail[4 + (half * 2 + part) * 2, j].astype(f32)
        return value + mail[4 + (half * 2 + 1 - part) * 2 + 1, j].astype(f32)

    def home(half, j):
        for part in range(2):
            if j == 2 or part == 1 - (j - 1) // 2:
                arrive(half, j, part)
                p_ref[home_at(half, j, part)] = total(half, j, part).astype(jnp.bfloat16)
                if j == 2:
                    second_copy(half, part, 0).start()
                else:
                    second_copy(half, 1 - part, 1).start()

    def after(c):
        send_place(c)
        for (half, w, j), at in CARRY_AT.items():
            if at == c:
                carry(half, w, j)
        for (half, j), at in HOME_AT.items():
            if at == c:
                home(half, j)
        if c == RELAY_AT:
            for copy in spread:
                copy.wait_recv()
            for copy in relay:
                copy.start()
        if c == HAND_AT:
            for copy in relay:
                copy.wait_recv()
            for copy in hand:
                copy.start()

    step(ORDER[0][0], ORDER[0][1], gb0, c0, rc0)

    def two(i, codes):
        cx, cy = codes
        step(lax.rem(cx, 4), lax.rem(cy, 4), gb1, c1, rc1)
        p_ref[2 * i] = multiply(gb0, c0, rc0)
        for place in range(8):
            @pl.when(i == place)
            def _():
                after(2 * place)
        cx, cy = cx // 4, cy // 4
        step(lax.rem(cx, 4), lax.rem(cy, 4), gb0, c0, rc0)
        p_ref[2 * i + 1] = multiply(gb1, c1, rc1)
        for place in range(8):
            @pl.when(i == place)
            def _():
                after(2 * place + 1)
        return cx // 4, cy // 4
    lax.fori_loop(0, 8, two, (jnp.int32(CODE[0] // 4), jnp.int32(CODE[1] // 4)))

    own_copy.wait()
    for copy in hand:
        copy.wait_recv()

    def load(i, slot):
        block = lax.rem(q + i + 1, 8)
        return pltpu.make_async_copy(all_ref.at[pl.ds(block * 2, 2)], mail.at[pl.ds(slot * 2, 2)], load_sem.at[slot])

    load(0, 0).start()
    load(1, 1).start()

    for half in range(2):
        for w in range(2):
            second_copy(half, w, 0).wait_recv()
            arrive(half, 1 + 2 * w, w)
            value = total(half, 1 + 2 * w, w) + near2[half, w].astype(f32)
            p_ref[home_at(half, 1 + 2 * w, w)] = value.astype(jnp.bfloat16)
            second_copy(half, w, 2).start()
    for half in range(2):
        for w in range(2):
            second_copy(half, w, 1).wait_recv()
            second_copy(half, w, 2).wait_recv()
        for w in range(2):
            rows = slice(256 * half + 128 * w, 256 * half + 128 * w + 128)
            arrive(half, 0, w)
            value = total(half, 0, w) + far2[half, w, 0].astype(f32) + far2[half, 1 - w, 1].astype(f32)
            hidden = jnp.maximum(value + bias_ref[...], 0.0)
            inv = lax.rsqrt(jnp.mean(hidden * hidden, axis=-1, keepdims=True) + 0.25)
            embed = (hidden * inv).astype(jnp.bfloat16)
            embed_ref[rows, :] = embed
            c0[rows, 0:512] = embed * jnp.bfloat16(0.25)
    for i in range(2, 6):
        load(i, i).start()

    def block_copy(d):
        return remote(stats.at[d - 1], got.at[q], send3.at[d - 1], recv3.at[d - 1], row_peers[d - 1])

    def block(i, _):
        slot = lax.rem(i, 6)
        load(i, slot).wait()
        for part in range(2):
            cols = pl.ds(part * 512, 512)
            scores = lax.dot_general(
                c0[:, 0:512], mail[2 * slot + part].reshape(512, 512), (((1,), (1,)), ((), ())),
                preferred_element_type=f32)
            scores = scores - jnp.concatenate([logc_ref[...]] * 4, axis=1)
            peak = jnp.max(scores, axis=0, keepdims=True)
            total = jnp.sum(jnp.exp(scores - peak), axis=0, keepdims=True)
            stats[i, 0:1, cols] = peak
            stats[i, 1:2, cols] = total
        for d in range(1, 8):
            @pl.when(i == d - 1)
            def _():
                block_copy(d).start()

        @pl.when(i < 2)
        def _():
            load(i + 6, slot).start()
        return 0
    lax.fori_loop(0, 8, block, 0)
    got[q] = stats[7]
    last_copies = [block_copy(d) for d in range(1, 8)]
    for copy in last_copies:
        copy.wait_recv()
    peak, total = joined(got[...])
    mine[...] = jnp.concatenate([peak, total], axis=0)
    final[me] = mine[...]
    for d, peer in enumerate(peers):
        last_copies.append(remote(mine, final.at[me], send4.at[d], recv4.at[d], peer))
        last_copies[-1].start()
    for copy in last_copies[7:]:
        copy.wait_recv()
    peak, total = joined(final[...])
    lse_ref[...] = peak + jnp.log(total) - math.log(65536)

    for copy in row_copies + aux_copies + spread + relay + hand + last_copies:
        copy.wait_send()
    for half in range(2):
        for w in range(2):
            for j in range(4):
                near_copy(half, w, j).wait_send()
                far_copy(half, w, 1, j).wait_send()
                far_copy(half, w, 2, j).wait_send()
            for stage in range(3):
                second_copy(half, w, stage).wait_send()


def joined(stats):
    peak = jnp.max(stats[:, 0:1, :], axis=0)
    total = jnp.sum(stats[:, 1:2, :] * jnp.exp(stats[:, 0:1, :] - peak[None]), axis=0)
    return peak, total


def tower(fetch_rows, slots, count, slot, table, wm, ws, wn, bm, bias, sampled, queries):
    any_space = pl.BlockSpec(memory_space=pl.ANY)
    bf16, f32, i32 = jnp.bfloat16, jnp.float32, jnp.int32
    dma = pltpu.SemaphoreType.DMA
    return pl.pallas_call(
        tower_kernel,
        out_shape=(
            jax.ShapeDtypeStruct((512, 512), bf16),
            jax.ShapeDtypeStruct((1, 1024), f32),
            jax.ShapeDtypeStruct((16, 4, 128, 512), bf16),
        ),
        in_specs=[VMEM] * 4 + [any_space] + [VMEM] * 6 + [any_space],
        out_specs=(VMEM, VMEM, any_space),
        scratch_shapes=[
            pltpu.VMEM((8192, 8, 128), f32),
            pltpu.VMEM((2, 512, 512), bf16),
            pltpu.VMEM((5120, 128), f32),
            pltpu.VMEM((640, 1024), bf16),
            pltpu.VMEM((640, 1024), bf16),
            pltpu.VMEM((512, 1280), bf16),
            pltpu.VMEM((512, 1280), bf16),
            pltpu.VMEM((512, 1), f32),
            pltpu.VMEM((512, 1), f32),
            pltpu.VMEM((48, 512), i32),
            pltpu.VMEM((48, 512), i32),
            pltpu.VMEM((512, 128), f32),
            pltpu.VMEM((512, 128), f32),
            pltpu.VMEM((16, 512, 512), bf16),
            pltpu.VMEM((16, 1, 640), i32),
            pltpu.VMEM((16, 1, 640), i32),
            pltpu.SMEM((10240,), i32),
            pltpu.VMEM((24, 512), i32),
            pltpu.VMEM((16, 24, 512), i32),
            pltpu.VMEM((12, 4, 128, 512), bf16),
            pltpu.VMEM((2, 2, 128, 512), bf16),
            pltpu.VMEM((2, 2, 2, 128, 512), bf16),
            pltpu.VMEM((512, 128), f32),
            pltpu.VMEM((8, 2, 1024), f32),
            pltpu.VMEM((8, 2, 1024), f32),
            pltpu.VMEM((2, 1024), f32),
            pltpu.VMEM((16, 2, 1024), f32),
            dma((2,)),
            dma((15,)), dma((15,)), dma((15,)), dma((15,)),
            dma((16,)), dma, dma((9,)), dma((9,)),
            dma((2, 2, 3, 4)), dma((2, 2, 3, 4)), dma((2, 2, 3)), dma((2, 2, 3)),
            dma((6,)), dma((7,)), dma((7,)), dma((15,)), dma((15,)),
        ],
        compiler_params=pltpu.CompilerParams(
            collective_id=1, has_side_effects=True, vmem_limit_bytes=67043328),
        name="tower",
    )(fetch_rows, slots, count, slot, table, wm, ws, wn, bm, bias, sampled, queries)


def per_device(
    items_table,
    fetch_rows,
    neighbour_slots,
    neighbour_count,
    self_slot,
    negative_count,
    message_weight,
    message_bias,
    self_weight,
    neighbour_weight,
    output_bias,
    queries,
):
    negative_embed, query_lse, _ = tower(
        fetch_rows, neighbour_slots.T, neighbour_count.reshape(1, 512), self_slot.reshape(1, 512), items_table,
        message_weight, self_weight, neighbour_weight, message_bias.reshape(1, 512), output_bias.reshape(1, 512),
        negative_count.reshape(1, 4096), queries.reshape(2, 4, 128, 512))
    return negative_embed, query_lse.reshape(1024)


def solution(mesh):
    in_specs = (
        P("neg", None),
        P(("neg", "qry"), None),
        P(("neg", "qry"), None),
        P(("neg", "qry")),
        P(("neg", "qry")),
        P("neg"),
        P(),
        P(),
        P(),
        P(),
        P(),
        P("qry", None),
    )
    out_specs = (P(("neg", "qry"), None), P("qry"))
    return jax.shard_map(
        per_device, mesh=mesh, in_specs=in_specs, out_specs=out_specs, check_vma=False
    )
```

time: 129 us -> 113 us (0.88)
  Pallas kernels: 122 us -> 109 us
  local copies, waits for them, and re-layouts: 5.1 us -> 3.13 us
    pallas_call x1 -> x0, Pallas kernels: 20.6 us -> none  [score(): pl.pallas_call(score_kernel, out_shape=(jax.ShapeDtypeStruct((512, 512),...]
    pallas_call x1, Pallas kernels: 102 us -> 109 us  [tower(): pl.pallas_call(tower_kernel, out_shape=(jax.ShapeDtypeStruct((512, 512),...]
    unnamed x8 -> x2, local copies, waits for them, and re-layouts: 4.24 us -> 3.13 us
where the time goes in v3:
time: 113 us
  Pallas kernels  109 us (96%)
  local copies, waits for them, and re-layouts  3.13 us (3%)
    pallas_call x1, Pallas kernels, tower(): pl.pallas_call(tower_kernel, out_shape=(jax.ShapeDtypeStruct((512, 512),...  109 us
    unnamed x2, local copies, waits for them, and re-layouts  3.13 us

profile of v3, /device:TPU:1, one launch (start us, length us, event | category | flops | bytes accessed | tf_op | source)
XLA Modules:
  0.0 112.7 jit_solution(9195012446589548823)
XLA Ops:
  0.6 108.9 %tower.1 = (bf16[512,512]{1,0:T(8,128)(2,1)}, f32[1,1024]{1,0:T(1,128)}, bf16[16,4,128,512]{3,2,1,0:T(8,128)(2,1)}) custom-call(s32[16,640]{1,0:T(8,128)} %fetch_ref.1, s32[40,512]{1,0:T(8,128)} %bitcast.9, s32[1,512]{1,0:T(1,128)} %bitcast.12, s32[1,512]{1,0:T(1,128)} %bitcast.13, bf16[8192,512]{1,0:T(8,128)(2,1)} %table_ref.1, bf16[512,512]{1,0:T(8,128)(2,1)} %wm_ref.1, ...), custom_call_target="tpu_custom_call" | custom-call | tf_op jit(solution)/shard_map/tower/pallas_call | solution.py:406
  109.5 1.9 %copy.16 = bf16[512,512]{1,0:T(8,128)(2,1)} copy(bf16[512,512]{1,0:T(8,128)(2,1)} %get-tuple-element.8) | data formatting | bytes 1048576
  111.4 1.3 %copy.17 = f32[1024]{0:T(1024)} copy(f32[1024]{0:T(1024)} %bitcast.11) | data formatting | bytes 8192

commit v4 on v3

--- a/solution.py
+++ b/solution.py
@@ -58,7 +58,7 @@
 GROUPS = ((0, 7), (7, 14), (14, 21), (21, 28), (28, 34), (34, 40))
 
 
-def prepare(n, p, rows_ref, aux_ref, t_ref, g_ref, self_ref, rcnt_ref, key_ref, val_ref, gb_ref, c_ref, rc_ref):
+def prepare(n, p, rows_ref, aux_ref, t_ref, g_ref, self_ref, rcnt_ref, key_ref, val_ref, gb_ref, c_ref, rc_ref, iota_ref):
     packed = aux_ref[n]
     for h, slots in enumerate((packed & 0xFFFF, lax.shift_right_logical(packed, 16))):
         rel = slots - 640 * p
@@ -73,7 +73,7 @@
     for vb in range(4):
         for s in range(vb * 160, vb * 160 + 160):
             r = rows_ref[n * 640 + s]
-            g_ref[s * 8:s * 8 + 8, :] = t_ref[r]
+            g_ref[s * 9:s * 9 + 8, :] = t_ref[r]
         cols = slice(vb * 128, (vb + 1) * 128)
         low = jnp.zeros((64, 128), jnp.int32)
         high = jnp.zeros((64, 128), jnp.int32)
@@ -83,7 +83,7 @@
                 kk = k if k < 20 else k + 4
                 key = jnp.broadcast_to(key_ref[kk:kk + 1, cols], (64, 128))
                 val = jnp.broadcast_to(val_ref[kk:kk + 1, cols], (64, 128))
-                acc = acc + jnp.where(sub == key, val, 0)
+                acc = acc + jnp.where(iota_ref[...] == key, val, 0)
             low = low + (acc & even)
             high = high + (lax.shift_right_logical(acc, 3) & even)
         ct = jnp.concatenate([low, high], axis=0).T
@@ -93,7 +93,7 @@
             c_ref[cols, f * 128:(f + 1) * 128] = (lax.shift_right_logical(ct, 6 * f) & 63).astype(jnp.float32).astype(jnp.bfloat16)
             c_ref[cols, 640 + f * 128:640 + (f + 1) * 128] = jnp.where(self_col == lane + f * 128, 1.0, 0.0).astype(jnp.bfloat16)
         for j in range(8):
-            gb_ref[vb * 160:vb * 160 + 160, j * 128:(j + 1) * 128] = g_ref[pl.ds(vb * 1280 + j, 160, stride=8), :].astype(jnp.bfloat16)
+            gb_ref[vb * 160:vb * 160 + 160, j * 128:(j + 1) * 128] = g_ref[pl.ds(vb * 1440 + j, 160, stride=9), :].astype(jnp.bfloat16)
 
 
 def multiply(gb_ref, c_ref, rc_ref):
@@ -115,12 +115,12 @@
 HOME_AT = {(0, 2): 8, (1, 2): 9, (1, 1): 13, (0, 1): 14, (0, 3): 14, (1, 3): 14}
 RELAY_AT, HAND_AT = 5, 12
 
-def tower_kernel(fetch_ref, slots_ref, count_ref, slot_ref, table_ref, wm_ref, ws_ref, wn_ref, bm_ref, bias_ref,
+def tower_kernel(fetch_ref, slots_ref, count_ref, slot_ref, table_ref, wm_in, ws_in, wn_in, bm_ref, bias_ref,
                  sampled_ref, queries_ref,
                  embed_ref, lse_ref, all_ref,
                  t_ref, tbuf, g_ref, gb0, gb1, c0, c1, rc0, rc1, key_ref, val_ref, self_ref, rcnt_ref, p_ref,
-                 rows_own, rows_got, rows_sm, aux_own, aux, mail, near2, far2, logc_ref, stats, got, mine, final,
-                 in_sem, row_send, row_recv, aux_send, aux_recv, sm_sem, own_sem, q_send, q_recv,
+                 wm_ref, ws_ref, wn_ref, iota_ref, rows_own, rows_got, rows_sm, aux_own, aux, mail, near2, far2, logc_ref, stats, got, mine, final,
+                 w_sem, in_sem, row_send, row_recv, aux_send, aux_recv, sm_sem, own_sem, q_send, q_recv,
                  send1, recv1, send2, recv2, load_sem, send3, recv3, send4, recv4):
     me = lax.axis_index("neg")
     q = lax.axis_index("qry")
@@ -134,6 +134,13 @@
         moved = lax.rem(spot[axis] + step + 4, 4)
         return {"neg": moved * 4 + spot[1] if axis == 0 else spot[0] * 4 + moved}
 
+    weights = [
+        pltpu.make_async_copy(source, target, w_sem.at[i])
+        for i, (source, target) in enumerate(((wm_in, wm_ref), (ws_in, ws_ref), (wn_in, wn_ref)))
+    ]
+    for copy in weights:
+        copy.start()
+    iota_ref[...] = lax.broadcasted_iota(jnp.int32, (64, 128), 0)
     for j in range(16):
         rows_own[j] = fetch_ref[j:j + 1, :]
     count = count_ref[...]
@@ -183,6 +190,8 @@
     for copy in spread:
         copy.start()
 
+    for copy in weights:
+        copy.wait()
     build_table(table_ref, wm_ref, ws_ref, wn_ref, bm_ref, t_ref, tbuf, in_sem)
 
     for copy in row_copies:
@@ -226,7 +235,7 @@
 
     def step(dx, dy, gb, c, rc):
         n = lax.rem(spot[0] + dx, 4) * 4 + lax.rem(spot[1] + dy, 4)
-        prepare(n, me, rows_sm, aux, t_ref, g_ref, self_ref, rcnt_ref, key_ref, val_ref, gb, c, rc)
+        prepare(n, me, rows_sm, aux, t_ref, g_ref, self_ref, rcnt_ref, key_ref, val_ref, gb, c, rc, iota_ref)
 
     f32 = jnp.float32
 
@@ -292,19 +301,24 @@
         cx, cy = codes
         step(lax.rem(cx, 4), lax.rem(cy, 4), gb1, c1, rc1)
         p_ref[2 * i] = multiply(gb0, c0, rc0)
-        for place in range(8):
+        for place in range(7):
             @pl.when(i == place)
             def _():
                 after(2 * place)
         cx, cy = cx // 4, cy // 4
         step(lax.rem(cx, 4), lax.rem(cy, 4), gb0, c0, rc0)
         p_ref[2 * i + 1] = multiply(gb1, c1, rc1)
-        for place in range(8):
+        for place in range(7):
             @pl.when(i == place)
             def _():
                 after(2 * place + 1)
         return cx // 4, cy // 4
-    lax.fori_loop(0, 8, two, (jnp.int32(CODE[0] // 4), jnp.int32(CODE[1] // 4)))
+    lax.fori_loop(0, 7, two, (jnp.int32(CODE[0] // 4), jnp.int32(CODE[1] // 4)))
+    step(ORDER[15][0], ORDER[15][1], gb1, c1, rc1)
+    p_ref[14] = multiply(gb0, c0, rc0)
+    after(14)
+    p_ref[15] = multiply(gb1, c1, rc1)
+    after(15)
 
     own_copy.wait()
     for copy in hand:
@@ -410,12 +424,12 @@
             jax.ShapeDtypeStruct((1, 1024), f32),
             jax.ShapeDtypeStruct((16, 4, 128, 512), bf16),
         ),
-        in_specs=[VMEM] * 4 + [any_space] + [VMEM] * 6 + [any_space],
+        in_specs=[VMEM] * 4 + [any_space] * 4 + [VMEM] * 3 + [any_space],
         out_specs=(VMEM, VMEM, any_space),
         scratch_shapes=[
             pltpu.VMEM((8192, 8, 128), f32),
             pltpu.VMEM((2, 512, 512), bf16),
-            pltpu.VMEM((5120, 128), f32),
+            pltpu.VMEM((5768, 128), f32),
             pltpu.VMEM((640, 1024), bf16),
             pltpu.VMEM((640, 1024), bf16),
             pltpu.VMEM((512, 1280), bf16),
@@ -427,6 +441,10 @@
             pltpu.VMEM((512, 128), f32),
             pltpu.VMEM((512, 128), f32),
             pltpu.VMEM((16, 512, 512), bf16),
+            pltpu.VMEM((512, 512), bf16),
+            pltpu.VMEM((512, 512), bf16),
+            pltpu.VMEM((512, 512), bf16),
+            pltpu.VMEM((64, 128), i32),
             pltpu.VMEM((16, 1, 640), i32),
             pltpu.VMEM((16, 1, 640), i32),
             pltpu.SMEM((10240,), i32),
@@ -440,7 +458,7 @@
             pltpu.VMEM((8, 2, 1024), f32),
             pltpu.VMEM((2, 1024), f32),
             pltpu.VMEM((16, 2, 1024), f32),
-            dma((2,)),
+            dma((3,)), dma((2,)),
             dma((15,)), dma((15,)), dma((15,)), dma((15,)),
             dma((16,)), dma, dma((9,)), dma((9,)),
             dma((2, 2, 3, 4)), dma((2, 2, 3, 4)), dma((2, 2, 3)), dma((2, 2, 3)),

time: 113 us -> 108 us (0.956)
  Pallas kernels: 109 us -> 103 us
    pallas_call x1, Pallas kernels: 109 us -> 103 us  [tower(): pl.pallas_call(tower_kernel, out_shape=(jax.ShapeDtypeStruct((512, 512),...]
where the time goes in v4:
time: 108 us; the launch traced here: 107 us
  Pallas kernels  103 us (95%)
  local copies, waits for them, and re-layouts  3.13 us (3%)
    pallas_call x1, Pallas kernels, tower(): pl.pallas_call(tower_kernel, out_shape=(jax.ShapeDtypeStruct((512, 512),...  103 us
    unnamed x2, local copies, waits for them, and re-layouts  3.13 us

profile of v4, /device:TPU:1, one launch (start us, length us, event | category | flops | bytes accessed | tf_op | source)
XLA Modules:
  0.0 107.2 jit_solution(13426815119737745473)
XLA Ops:
  0.6 103.4 %tower.1 = (bf16[512,512]{1,0:T(8,128)(2,1)}, f32[1,1024]{1,0:T(1,128)}, bf16[16,4,128,512]{3,2,1,0:T(8,128)(2,1)}) custom-call(s32[16,640]{1,0:T(8,128)} %fetch_ref.1, s32[40,512]{1,0:T(8,128)} %bitcast.9, s32[1,512]{1,0:T(1,128)} %bitcast.12, s32[1,512]{1,0:T(1,128)} %bitcast.13, bf16[8192,512]{1,0:T(8,128)(2,1)} %table_ref.1, bf16[512,512]{1,0:T(8,128)(2,1)} %wm_in.1, ...), custom_call_target="tpu_custom_call" | custom-call | tf_op jit(solution)/shard_map/tower/pallas_call | solution.py:420
  104.0 1.9 %copy.16 = bf16[512,512]{1,0:T(8,128)(2,1)} copy(bf16[512,512]{1,0:T(8,128)(2,1)} %get-tuple-element.8) | data formatting | bytes 1048576
  105.9 1.3 %copy.17 = f32[1024]{0:T(1024)} copy(f32[1024]{0:T(1024)} %bitcast.11) | data formatting | bytes 8192

commit v5 on v4

--- a/solution.py
+++ b/solution.py
@@ -12,47 +12,64 @@
 VMEM = pl.BlockSpec(memory_space=pltpu.VMEM)
 
 
-def greet(peers):
-    barrier = pltpu.get_barrier_semaphore()
-    for peer in peers:
-        pl.semaphore_signal(barrier, inc=1, device_id=peer, device_id_type=MESH)
-    pl.semaphore_wait(barrier, len(peers))
-
-
 def remote(src, dst, send, recv, peer):
     return pltpu.make_async_remote_copy(
         src_ref=src, dst_ref=dst, send_sem=send, recv_sem=recv, device_id=peer, device_id_type=MESH
     )
 
 
-def build_table(table_ref, wm_ref, ws_ref, wn_ref, bm_ref, t_ref, tbuf, in_sem):
+def build_table(table_ref, wm_ref, ws_ref, wn_ref, bm_ref, t_ref, tbuf, spare, m_ref, in_sem):
     blk = 512
-    blocks = 16
+    flat = t_ref.reshape(65536, 128)
 
     def fetch(i, slot):
-        return pltpu.make_async_copy(table_ref.at[pl.ds(i * blk, blk), :], tbuf.at[slot], in_sem.at[slot])
-
-    fetch(0, 0).start()
+        target = tbuf.at[slot] if slot < 2 else spare.at[0:512, (slot - 2) * 512:(slot - 1) * 512]
+        return pltpu.make_async_copy(table_ref.at[pl.ds(i * blk, blk), :], target, in_sem.at[slot])
+
+    def dot(x, w_ref):
+        return jnp.dot(x, w_ref[...], preferred_element_type=jnp.float32)
+
+    def message(x):
+        return jnp.maximum(dot(x, wm_ref) + bm_ref[...], 0.0).astype(jnp.bfloat16)
+
+    def put(i, first, value):
+        base = pl.multiple_of(i * (blk * 8), 8)
+        for j in range(4):
+            flat[pl.ds(base + first + j, blk, stride=8), :] = value[:, j * 128:(j + 1) * 128]
+
+
+    def pair(i, slot, carried):
+        fetch(2 * i, slot).wait()
+        fetch(2 * i + 1, slot + 1).wait()
+        if slot == 0:
+            x, y = tbuf[0], tbuf[1]
+        else:
+            x, y = spare[0:512, 0:512], spare[0:512, 512:1024]
+        if carried:
+            before = m_ref[:, 0:512]
+        mx = message(x)
+        if carried:
+            put(jnp.maximum(2 * i - 1, 0), 0, dot(before, wn_ref))
+        put(2 * i, 4, dot(x, ws_ref))
+        my = message(y)
+        put(2 * i, 0, dot(mx, wn_ref))
+        put(2 * i + 1, 4, dot(y, ws_ref))
+        m_ref[:, 0:512] = my
 
     def build(i, _):
-        slot = lax.rem(i, 2)
-
-        @pl.when(i + 1 < blocks)
+        fetch(4 * i + 2, 2).start()
+        fetch(4 * i + 3, 3).start()
+        pair(2 * i, 0, True)
+
+        @pl.when(i < 3)
         def _():
-            fetch(i + 1, 1 - slot).start()
-        fetch(i, slot).wait()
-        x = tbuf[slot]
-        m = jnp.dot(x, wm_ref[...], preferred_element_type=jnp.float32) + bm_ref[...]
-        m = jnp.maximum(m, 0.0).astype(jnp.bfloat16)
-        t1 = jnp.dot(m, wn_ref[...], preferred_element_type=jnp.float32)
-        t2 = jnp.dot(x, ws_ref[...], preferred_element_type=jnp.float32)
-        base = pl.multiple_of(i * (blk * 8), 8)
-        flat = t_ref.reshape(65536, 128)
-        for j in range(4):
-            flat[pl.ds(base + j, blk, stride=8), :] = t1[:, j * 128:(j + 1) * 128]
-            flat[pl.ds(base + 4 + j, blk, stride=8), :] = t2[:, j * 128:(j + 1) * 128]
+            fetch(4 * i + 4, 0).start()
+            fetch(4 * i + 5, 1).start()
+        pair(2 * i + 1, 2, True)
         return 0
-    lax.fori_loop(0, blocks, build, 0)
+    m_ref[:, 0:512] = jnp.zeros((512, 512), jnp.bfloat16)
+    lax.fori_loop(0, 4, build, 0)
+    put(15, 0, dot(m_ref[:, 0:512], wn_ref))
 
 
 GROUPS = ((0, 7), (7, 14), (14, 21), (21, 28), (28, 34), (34, 40))
@@ -112,7 +129,7 @@
     (0, 0, 2): 3, (0, 1, 2): 3, (1, 0, 2): 4, (1, 1, 2): 4, (0, 0, 1): 7, (0, 1, 1): 10, (0, 0, 3): 9, (0, 1, 3): 8,
     (1, 0, 1): 6, (1, 1, 1): 9, (1, 0, 3): 10, (1, 1, 3): 7, (0, 0, 0): 11, (0, 1, 0): 13, (1, 0, 0): 12, (1, 1, 0): 14,
 }
-HOME_AT = {(0, 2): 8, (1, 2): 9, (1, 1): 13, (0, 1): 14, (0, 3): 14, (1, 3): 14}
+HOME_AT = {(0, 2): 8, (1, 2): 9, (1, 1): 13, (0, 1): 15, (0, 3): 15, (1, 3): 15}
 RELAY_AT, HAND_AT = 5, 12
 
 def tower_kernel(fetch_ref, slots_ref, count_ref, slot_ref, table_ref, wm_in, ws_in, wn_in, bm_ref, bias_ref,
@@ -140,6 +157,12 @@
     ]
     for copy in weights:
         copy.start()
+    for i in range(2):
+        pltpu.make_async_copy(table_ref.at[pl.ds(i * 512, 512), :], tbuf.at[i], in_sem.at[i]).start()
+    row_peers = [{"qry": lax.rem(q + d, 8)} for d in range(1, 8)]
+    barrier = pltpu.get_barrier_semaphore()
+    for peer in peers + row_peers:
+        pl.semaphore_signal(barrier, inc=1, device_id=peer, device_id_type=MESH)
     iota_ref[...] = lax.broadcasted_iota(jnp.int32, (64, 128), 0)
     for j in range(16):
         rows_own[j] = fetch_ref[j:j + 1, :]
@@ -153,11 +176,7 @@
             aux_own[0:20, :] = low | jnp.left_shift(half, 16)
     aux_own[20:24, :] = jnp.broadcast_to(slot_ref[...] | jnp.left_shift(count, 16), (4, 512))
 
-    sampled = sampled_ref[:, pl.ds(pl.multiple_of(q * 512, 128), 512)].astype(jnp.float32)
-    logc_ref[...] = jnp.broadcast_to(jnp.log(sampled), (128, 512)).T
-
-    row_peers = [{"qry": lax.rem(q + d, 8)} for d in range(1, 8)]
-    greet(peers + row_peers)
+    pl.semaphore_wait(barrier, len(peers + row_peers))
     row_copies = []
     aux_copies = []
     for d, peer in enumerate(peers):
@@ -190,9 +209,12 @@
     for copy in spread:
         copy.start()
 
+    sampled = sampled_ref[:, pl.ds(pl.multiple_of(q * 512, 128), 512)].astype(jnp.float32)
+    logc_ref[...] = jnp.broadcast_to(jnp.log(sampled), (128, 512)).T
+
     for copy in weights:
         copy.wait()
-    build_table(table_ref, wm_ref, ws_ref, wn_ref, bm_ref, t_ref, tbuf, in_sem)
+    build_table(table_ref, wm_ref, ws_ref, wn_ref, bm_ref, t_ref, tbuf, gb1, c0, in_sem)
 
     for copy in row_copies:
         copy.wait_recv()
@@ -458,7 +480,7 @@
             pltpu.VMEM((8, 2, 1024), f32),
             pltpu.VMEM((2, 1024), f32),
             pltpu.VMEM((16, 2, 1024), f32),
-            dma((3,)), dma((2,)),
+            dma((3,)), dma((4,)),
             dma((15,)), dma((15,)), dma((15,)), dma((15,)),
             dma((16,)), dma, dma((9,)), dma((9,)),
             dma((2, 2, 3, 4)), dma((2, 2, 3, 4)), dma((2, 2, 3)), dma((2, 2, 3)),

time: 108 us -> 106 us (0.981)
    pallas_call x1, Pallas kernels: 103 us -> 102 us  [tower(): pl.pallas_call(tower_kernel, out_shape=(jax.ShapeDtypeStruct((512, 512),...]
where the time goes in v5:
time: 106 us; the launch traced here: 105 us
  Pallas kernels  102 us (96%)
  local copies, waits for them, and re-layouts  3.13 us (3%)
    pallas_call x1, Pallas kernels, tower(): pl.pallas_call(tower_kernel, out_shape=(jax.ShapeDtypeStruct((512, 512),...  102 us
    unnamed x2, local copies, waits for them, and re-layouts  3.13 us

profile of v5, /device:TPU:1, one launch (start us, length us, event | category | flops | bytes accessed | tf_op | source)
XLA Modules:
  0.0 105.5 jit_solution(9628783752559204780)
XLA Ops:
  0.6 101.7 %tower.1 = (bf16[512,512]{1,0:T(8,128)(2,1)}, f32[1,1024]{1,0:T(1,128)}, bf16[16,4,128,512]{3,2,1,0:T(8,128)(2,1)}) custom-call(s32[16,640]{1,0:T(8,128)} %fetch_ref.1, s32[40,512]{1,0:T(8,128)} %bitcast.9, s32[1,512]{1,0:T(1,128)} %bitcast.12, s32[1,512]{1,0:T(1,128)} %bitcast.13, bf16[8192,512]{1,0:T(8,128)(2,1)} %table_ref.1, bf16[512,512]{1,0:T(8,128)(2,1)} %wm_in.1, ...), custom_call_target="tpu_custom_call" | custom-call | tf_op jit(solution)/shard_map/tower/pallas_call | solution.py:442
  102.4 1.9 %copy.16 = bf16[512,512]{1,0:T(8,128)(2,1)} copy(bf16[512,512]{1,0:T(8,128)(2,1)} %get-tuple-element.8) | data formatting | bytes 1048576
  104.2 1.3 %copy.17 = f32[1024]{0:T(1024)} copy(f32[1024]{0:T(1024)} %bitcast.11) | data formatting | bytes 8192

commit v6 on v5

--- a/solution.py
+++ b/solution.py
@@ -321,24 +321,24 @@
 
     def two(i, codes):
         cx, cy = codes
-        step(lax.rem(cx, 4), lax.rem(cy, 4), gb1, c1, rc1)
         p_ref[2 * i] = multiply(gb0, c0, rc0)
         for place in range(7):
             @pl.when(i == place)
             def _():
                 after(2 * place)
+        step(lax.rem(cx, 4), lax.rem(cy, 4), gb1, c1, rc1)
         cx, cy = cx // 4, cy // 4
-        step(lax.rem(cx, 4), lax.rem(cy, 4), gb0, c0, rc0)
         p_ref[2 * i + 1] = multiply(gb1, c1, rc1)
         for place in range(7):
             @pl.when(i == place)
             def _():
                 after(2 * place + 1)
+        step(lax.rem(cx, 4), lax.rem(cy, 4), gb0, c0, rc0)
         return cx // 4, cy // 4
     lax.fori_loop(0, 7, two, (jnp.int32(CODE[0] // 4), jnp.int32(CODE[1] // 4)))
-    step(ORDER[15][0], ORDER[15][1], gb1, c1, rc1)
     p_ref[14] = multiply(gb0, c0, rc0)
     after(14)
+    step(ORDER[15][0], ORDER[15][1], gb1, c1, rc1)
     p_ref[15] = multiply(gb1, c1, rc1)
     after(15)
 

time: 106 us -> 104 us (0.981)
  Pallas kernels: 102 us -> 99.7 us
    pallas_call x1, Pallas kernels: 102 us -> 99.7 us  [tower(): pl.pallas_call(tower_kernel, out_shape=(jax.ShapeDtypeStruct((512, 512),...]
where the time goes in v6:
time: 104 us; the launch traced here: 103 us
  Pallas kernels  99.7 us (96%)
  local copies, waits for them, and re-layouts  3.13 us (3%)
    pallas_call x1, Pallas kernels, tower(): pl.pallas_call(tower_kernel, out_shape=(jax.ShapeDtypeStruct((512, 512),...  99.7 us
    unnamed x2, local copies, waits for them, and re-layouts  3.13 us

profile of v6, /device:TPU:1, one launch (start us, length us, event | category | flops | bytes accessed | tf_op | source)
XLA Modules:
  0.0 103.4 jit_solution(9738051205401332144)
XLA Ops:
  0.6 99.7 %tower.1 = (bf16[512,512]{1,0:T(8,128)(2,1)}, f32[1,1024]{1,0:T(1,128)}, bf16[16,4,128,512]{3,2,1,0:T(8,128)(2,1)}) custom-call(s32[16,640]{1,0:T(8,128)} %fetch_ref.1, s32[40,512]{1,0:T(8,128)} %bitcast.9, s32[1,512]{1,0:T(1,128)} %bitcast.12, s32[1,512]{1,0:T(1,128)} %bitcast.13, bf16[8192,512]{1,0:T(8,128)(2,1)} %table_ref.1, bf16[512,512]{1,0:T(8,128)(2,1)} %wm_in.1, ...), custom_call_target="tpu_custom_call" | custom-call | tf_op jit(solution)/shard_map/tower/pallas_call | solution.py:442
  100.3 1.9 %copy.16 = bf16[512,512]{1,0:T(8,128)(2,1)} copy(bf16[512,512]{1,0:T(8,128)(2,1)} %get-tuple-element.8) | data formatting | bytes 1048576
  102.2 1.3 %copy.17 = f32[1024]{0:T(1024)} copy(f32[1024]{0:T(1024)} %bitcast.11) | data formatting | bytes 8192
